TPU v7x, 32 devices: a whole 2x2x4 slice. The times are simulated.
32 devices in a mesh: fsdp: 2 (over x), ctx: 4 (over y, core), tp: 4 (over z).
Axes of the slice: x: 2, y: 2, z: 4, core: 2. Of those that a mesh axis runs over, the one named last changes fastest.
Arguments:
- tokens: bfloat16 [8, 1024, 2048], P('fsdp', 'ctx'), may hold values from -8 to 8
- positions: int32 [8, 1024], P('fsdp', 'ctx'), may hold values from 0 to 383, as said below
- block_ids: int32 [8, 1024], P('fsdp', 'ctx'), may hold values from 0 to 3, as said below
- gain_attend: bfloat16 [2048], P('fsdp'), may hold values from 0.099609375 to 1.8984375
- w_query: bfloat16 [2048, 2048], P('fsdp', 'tp'), may hold values from -0.125 to 0.125
- w_key: bfloat16 [2048, 2048], P('fsdp', 'tp'), may hold values from -0.125 to 0.125
- w_value: bfloat16 [2048, 2048], P('fsdp', 'tp'), may hold values from -0.125 to 0.125
- w_output: bfloat16 [2048, 2048], P('tp', 'fsdp'), may hold values from -1 to 1
- gain_feed: bfloat16 [2048], P('fsdp'), may hold values from 0.099609375 to 1.8984375
- w_gate: bfloat16 [2048, 8192], P('fsdp', 'tp'), may hold values from -0.125 to 0.125
- w_up: bfloat16 [2048, 8192], P('fsdp', 'tp'), may hold values from -0.125 to 0.125
- w_down: bfloat16 [8192, 2048], P('tp', 'fsdp'), may hold values from -0.0625 to 0.0625
- cotangent: bfloat16 [8, 1024, 2048], P('fsdp', 'ctx'), may hold values from -6 to 6
Outputs:
- layer_out: bfloat16 [8, 1024, 2048], P('fsdp', 'ctx')
- grad_input: bfloat16 [8, 1024, 2048], P('fsdp', 'ctx')
- grad_gain_attend: float32 [2048], P(('fsdp', 'ctx'))
- grad_w_query: float32 [2048, 2048], P(('fsdp', 'ctx'), 'tp')
- grad_w_key: float32 [2048, 2048], P(('fsdp', 'ctx'), 'tp')
- grad_w_value: float32 [2048, 2048], P(('fsdp', 'ctx'), 'tp')
- grad_w_output: float32 [2048, 2048], P('tp', ('fsdp', 'ctx'))
- grad_gain_feed: float32 [2048], P(('fsdp', 'ctx'))
- grad_w_gate: float32 [2048, 8192], P(('fsdp', 'ctx'), 'tp')
- grad_w_up: float32 [2048, 8192], P(('fsdp', 'ctx'), 'tp')
- grad_w_down: float32 [8192, 2048], P('tp', ('fsdp', 'ctx'))
- stream_rms: float32 [], replicated
- attend_rms: float32 [], replicated
- feed_rms: float32 [], replicated
Inputs may be any that keep to these rules, and one draw needn't show every extreme that they name: Along each sequence, positions count 0, 1, 2 and so on from the first token of each block, a run of equal block ids. `block_ids`: along each sequence block ids start at 0, never fall and rise by one at each new block.
All inputs are finite; a program needn't handle non-finite values.
Results may differ from a plain program's by a relative error of at most 0.015.
Values may be sent and summed in bfloat16 or wider, within the bound.
A program may use at most 256 MiB of HBM per device.

v0:
```python
import math

import jax
import jax.numpy as jnp
from jax import lax
from jax.sharding import PartitionSpec as P

HD = 128


norm_epsilon = 1e-05
rope_base = 10000.0


def plain_dot(left_side, right_side):
    return jnp.dot(left_side, right_side, preferred_element_type=jnp.float32)


def dot_last(left_side, right_side):
    return lax.dot_general(
        left_side, right_side, (((1,), (1,)), ((), ())), preferred_element_type=jnp.float32
    )


def dot_first(left_side, right_side):
    return lax.dot_general(
        left_side, right_side, (((0,), (0,)), ((), ())), preferred_element_type=jnp.float32
    )


def inverse_rms(values):
    return lax.rsqrt(jnp.mean(values * values, axis=-1, keepdims=True) + norm_epsilon)


def norm_back(grad_norm, values, scale_rows, gain):
    weighted = grad_norm * gain
    inner_mean = jnp.mean(weighted * values, axis=-1, keepdims=True)
    grad_values = (
        scale_rows * weighted - values * (scale_rows * scale_rows * scale_rows) * inner_mean
    )
    grad_gain = jnp.sum(grad_norm * (values * scale_rows), axis=0)
    return (grad_values, grad_gain)


def rope_tables(positions, head_size):
    half_size = head_size // 2
    inverse = jnp.exp(
        jnp.arange(half_size, dtype=jnp.float32) * (-2.0 * math.log(rope_base) / head_size)
    )
    turned = positions.astype(jnp.float32)[..., None, None] * inverse
    return (jnp.cos(turned), jnp.sin(turned))


def rotate(values, cosine, sine_table, direction):
    half_size = values.shape[-1] // 2
    first_half = values[..., :half_size]
    second_half = values[..., half_size:]
    return jnp.concatenate(
        [
            first_half * cosine - direction * (second_half * sine_table),
            direction * (first_half * sine_table) + second_half * cosine,
        ],
        axis=-1,
    )


def local(
    tokens,
    positions,
    block_ids,
    gain_attend,
    w_query,
    w_key,
    w_value,
    w_output,
    gain_feed,
    w_gate,
    w_up,
    w_down,
    cotangent,
):
    seq_count, block_len, model_width = tokens.shape
    row_count = seq_count * block_len
    seq_len = block_len * lax.axis_size("ctx")
    heads_here = w_query.shape[1] // HD
    score_scale = 1.0 / math.sqrt(HD)
    score_shift = math.log(seq_len)
    shape_heads = (seq_count, block_len, heads_here, HD)
    stream = tokens.reshape(row_count, model_width).astype(jnp.float32)
    query_full, key_full, value_full, output_full, gain_one = (
        lax.all_gather(w_query, "fsdp", axis=0, tiled=True),
        lax.all_gather(w_key, "fsdp", axis=0, tiled=True),
        lax.all_gather(w_value, "fsdp", axis=0, tiled=True),
        lax.all_gather(w_output, "fsdp", axis=1, tiled=True),
        lax.all_gather(gain_attend, "fsdp", axis=0, tiled=True),
    )
    gain_one = gain_one.astype(jnp.float32)
    scale_one = inverse_rms(stream)
    normed_one = (stream * scale_one * gain_one).astype(jnp.bfloat16)
    queries = plain_dot(normed_one, query_full)
    key_proj = plain_dot(normed_one, key_full)
    values = plain_dot(normed_one, value_full).astype(jnp.bfloat16)
    cosine, sine_table = rope_tables(positions, HD)
    query_rot = rotate(queries.reshape(shape_heads), cosine, sine_table, 1.0).astype(jnp.bfloat16)
    key_rot = (
        rotate(key_proj.reshape(shape_heads), cosine, sine_table, 1.0)
        .astype(jnp.bfloat16)
        .reshape(seq_count, block_len, heads_here * HD)
    )
    value_rows = values.reshape(seq_count, block_len, heads_here * HD)
    query_tags = block_ids.astype(jnp.float32)
    key_tags = block_ids.astype(jnp.bfloat16)

    def scores_of(portion):
        key_piece, value_piece, tag_piece = portion
        span = key_piece.shape[1]
        key_heads = key_piece.reshape(seq_count, span, heads_here, HD)
        value_heads = value_piece.reshape(seq_count, span, heads_here, HD)
        logits = (
            jnp.einsum("sqhd,skhd->shqk", query_rot, key_heads, preferred_element_type=jnp.float32)
            * score_scale
            - score_shift
        )
        allowed = tag_piece.astype(jnp.float32)[:, None, None, :] <= query_tags[:, None, :, None]
        return (key_heads, value_heads, jax.nn.sigmoid(logits), allowed)

    key_heads, value_heads, squashed, allowed = scores_of(
        (
            lax.all_gather(key_rot, "ctx", axis=1, tiled=True),
            lax.all_gather(value_rows, "ctx", axis=1, tiled=True),
            lax.all_gather(key_tags, "ctx", axis=1, tiled=True),
        )
    )
    weights = jnp.where(allowed, squashed, 0.0).astype(jnp.bfloat16)
    attended = jnp.einsum(
        "shqk,skhd->sqhd", weights, value_heads, preferred_element_type=jnp.float32
    )
    mixed_rows = attended.reshape(row_count, heads_here * HD).astype(jnp.bfloat16)
    attend_out = lax.psum(plain_dot(mixed_rows, output_full), "tp")
    middle = stream + attend_out
    gate_full, up_full, down_full, gain_two = (
        lax.all_gather(w_gate, "fsdp", axis=0, tiled=True),
        lax.all_gather(w_up, "fsdp", axis=0, tiled=True),
        lax.all_gather(w_down, "fsdp", axis=1, tiled=True),
        lax.all_gather(gain_feed, "fsdp", axis=0, tiled=True),
    )
    gain_two = gain_two.astype(jnp.float32)
    scale_two = inverse_rms(middle)
    normed_two = (middle * scale_two * gain_two).astype(jnp.bfloat16)
    gate_vals = plain_dot(normed_two, gate_full)
    up_vals = plain_dot(normed_two, up_full)
    gate_sig = jax.nn.sigmoid(gate_vals)
    gate_act = gate_vals * gate_sig
    hidden = (gate_act * up_vals).astype(jnp.bfloat16)
    feed_out = lax.psum(plain_dot(hidden, down_full), "tp")
    result = middle + feed_out
    layer_out = result.astype(jnp.bfloat16).reshape(tokens.shape)
    totals = lax.psum(
        (jnp.sum(result * result), jnp.sum(attend_out * attend_out), jnp.sum(feed_out * feed_out)),
        ("fsdp", "ctx"),
    )
    entries = float(row_count * model_width * lax.axis_size("fsdp") * lax.axis_size("ctx"))
    stream_rms = jnp.sqrt(totals[0] / entries)
    attend_rms = jnp.sqrt(totals[1] / entries)
    feed_rms = jnp.sqrt(totals[2] / entries)
    query_full, key_full, value_full, output_full, gate_full, up_full, down_full = (
        lax.all_gather(w_query, "fsdp", axis=0, tiled=True),
        lax.all_gather(w_key, "fsdp", axis=0, tiled=True),
        lax.all_gather(w_value, "fsdp", axis=0, tiled=True),
        lax.all_gather(w_output, "fsdp", axis=1, tiled=True),
        lax.all_gather(w_gate, "fsdp", axis=0, tiled=True),
        lax.all_gather(w_up, "fsdp", axis=0, tiled=True),
        lax.all_gather(w_down, "fsdp", axis=1, tiled=True),
    )
    grad_rows = cotangent.reshape(row_count, model_width)
    grad_stream = grad_rows.astype(jnp.float32)
    grad_hidden = dot_last(grad_rows, down_full)
    grad_down = dot_first(hidden, grad_rows)
    slope = gate_sig * (1.0 + gate_vals * (1.0 - gate_sig))
    grad_gate = (grad_hidden * up_vals * slope).astype(jnp.bfloat16)
    grad_up = (grad_hidden * gate_act).astype(jnp.bfloat16)
    grad_normed_two = lax.psum(dot_last(grad_gate, gate_full) + dot_last(grad_up, up_full), "tp")
    grad_gate_w = dot_first(normed_two, grad_gate)
    grad_up_w = dot_first(normed_two, grad_up)
    grad_middle_norm, grad_gain_two = norm_back(grad_normed_two, middle, scale_two, gain_two)
    grad_middle = grad_stream + grad_middle_norm
    grad_attend = grad_middle.astype(jnp.bfloat16)
    grad_mixed = dot_last(grad_attend, output_full).astype(jnp.bfloat16)
    grad_output_w = dot_first(mixed_rows, grad_attend)
    grad_mixed_heads = grad_mixed.reshape(shape_heads)
    key_heads, value_heads, squashed, allowed = scores_of(
        (
            lax.all_gather(key_rot, "ctx", axis=1, tiled=True),
            lax.all_gather(value_rows, "ctx", axis=1, tiled=True),
            lax.all_gather(key_tags, "ctx", axis=1, tiled=True),
        )
    )
    span = key_heads.shape[1]
    weights = jnp.where(allowed, squashed, 0.0).astype(jnp.bfloat16)
    grad_weights = jnp.einsum(
        "sqhd,skhd->shqk", grad_mixed_heads, value_heads, preferred_element_type=jnp.float32
    )
    grad_logits = jnp.where(allowed, grad_weights * squashed * (1.0 - squashed), 0.0).astype(
        jnp.bfloat16
    )
    grad_query = score_scale * jnp.einsum(
        "shqk,skhd->sqhd", grad_logits, key_heads, preferred_element_type=jnp.float32
    )
    key_part = (
        score_scale
        * jnp.einsum("shqk,sqhd->skhd", grad_logits, query_rot, preferred_element_type=jnp.float32)
    ).reshape(seq_count, span, heads_here * HD)
    value_part = jnp.einsum(
        "shqk,sqhd->skhd", weights, grad_mixed_heads, preferred_element_type=jnp.float32
    ).reshape(seq_count, span, heads_here * HD)
    grad_key_mine, grad_value_mine = (
        lax.psum_scatter(key_part, "ctx", scatter_dimension=1, tiled=True),
        lax.psum_scatter(value_part, "ctx", scatter_dimension=1, tiled=True),
    )
    grad_query_rows = (
        rotate(grad_query, cosine, sine_table, -1.0)
        .reshape(row_count, heads_here * HD)
        .astype(jnp.bfloat16)
    )
    grad_key_rows = (
        rotate(grad_key_mine.reshape(shape_heads), cosine, sine_table, -1.0)
        .reshape(row_count, heads_here * HD)
        .astype(jnp.bfloat16)
    )
    grad_value_rows = grad_value_mine.reshape(row_count, heads_here * HD).astype(jnp.bfloat16)
    grad_normed_one = lax.psum(
        dot_last(grad_query_rows, query_full)
        + dot_last(grad_key_rows, key_full)
        + dot_last(grad_value_rows, value_full),
        "tp",
    )
    grad_query_w = dot_first(normed_one, grad_query_rows)
    grad_key_w = dot_first(normed_one, grad_key_rows)
    grad_value_w = dot_first(normed_one, grad_value_rows)
    grad_input_norm, grad_gain_one = norm_back(grad_normed_one, stream, scale_one, gain_one)
    grad_input = (grad_middle + grad_input_norm).astype(jnp.bfloat16).reshape(tokens.shape)
    summed = (
        lax.psum_scatter(grad_gain_one, ("fsdp", "ctx"), scatter_dimension=0, tiled=True),
        lax.psum_scatter(grad_query_w, ("fsdp", "ctx"), scatter_dimension=0, tiled=True),
        lax.psum_scatter(grad_key_w, ("fsdp", "ctx"), scatter_dimension=0, tiled=True),
        lax.psum_scatter(grad_value_w, ("fsdp", "ctx"), scatter_dimension=0, tiled=True),
        lax.psum_scatter(grad_output_w, ("fsdp", "ctx"), scatter_dimension=1, tiled=True),
        lax.psum_scatter(grad_gain_two, ("fsdp", "ctx"), scatter_dimension=0, tiled=True),
        lax.psum_scatter(grad_gate_w, ("fsdp", "ctx"), scatter_dimension=0, tiled=True),
        lax.psum_scatter(grad_up_w, ("fsdp", "ctx"), scatter_dimension=0, tiled=True),
        lax.psum_scatter(grad_down, ("fsdp", "ctx"), scatter_dimension=1, tiled=True),
    )
    return (
        layer_out,
        grad_input,
        summed[0],
        summed[1],
        summed[2],
        summed[3],
        summed[4],
        summed[5],
        summed[6],
        summed[7],
        summed[8],
        stream_rms,
        attend_rms,
        feed_rms,
    )


def solution(mesh):
    placed = (
        P("fsdp", "ctx", None),
        P("fsdp", "ctx"),
        P("fsdp", "ctx"),
        P("fsdp"),
        P("fsdp", "tp"),
        P("fsdp", "tp"),
        P("fsdp", "tp"),
        P("tp", "fsdp"),
        P("fsdp"),
        P("fsdp", "tp"),
        P("fsdp", "tp"),
        P("tp", "fsdp"),
        P("fsdp", "ctx", None),
    )
    return jax.shard_map(
        local,
        mesh=mesh,
        in_specs=placed,
        out_specs=(
            P("fsdp", "ctx", None),
            P("fsdp", "ctx", None),
            P(("fsdp", "ctx")),
            P(("fsdp", "ctx"), "tp"),
            P(("fsdp", "ctx"), "tp"),
            P(("fsdp", "ctx"), "tp"),
            P("tp", ("fsdp", "ctx")),
            P(("fsdp", "ctx")),
            P(("fsdp", "ctx"), "tp"),
            P(("fsdp", "ctx"), "tp"),
            P("tp", ("fsdp", "ctx")),
            P(),
            P(),
            P(),
        ),
        check_vma=False,
    )
```

profile of v0, /device:TPU:0, one launch (start us, length us, event | category | flops | bytes accessed | tf_op | source)
XLA Modules:
  0.0 2545.2 jit_solution(7070096330234557118)
XLA Ops:
  9.4 5.5 all_gather.46
  14.9 3.1 fusion.4
  18.7 5.6 fusion.6
  25.4 20.0 all-gather.16.cloned.1.call-done
  45.4 2.9 copy.52
  48.3 31.7 %all-gather.14.cloned.1.call-done = bf16[2048,512]{1,0:T(8,128)(2,1)} async-done(((bf16[1024,512]{1,0:T(8,128)(2,1)}), bf16[2048,512]{1,0:T(8,128)(2,1)}) %all-gather.14.cloned.1.call-update) | async-done | bytes 2097168 | tf_op jit(solution)/shard_map/all_gather | solution.py:91
  80.0 3.9 copy.51
  84.0 4.7 fusion.13
  93.1 5.2 fusion.2
  98.3 16.4 all-gather.10.cloned.1.call-done
  114.7 6.2 convolution_convert_fusion
  121.6 5.4 all_gather.49
  127.6 24.1 all-gather.18.cloned.1.call-done
  151.7 11.6 add_divide_fusion
  163.3 24.9 all-gather.12.cloned.1.call-done
  188.2 6.2 copy.50
  194.4 11.0 fusion.27
  206.1 16.6 all-gather.20.cloned.1.call-done
  222.7 7.2 fusion.37
  232.1 4.8 all_gather.54
  236.9 284.1 %all-reduce.8.cloned.1.call-done = f32[1024,2048]{1,0:T(8,128)} async-done(((f32[1024,2048]{1,0:T(8,128)}), f32[1024,2048]{1,0:T(8,128)}) %all-reduce.8.cloned.1.call-update) | async-done | bytes 8388624 | tf_op jit(solution)/shard_map/psum | solution.py:139
  520.9 7.6 multiply_reduce_fusion.5
  528.5 4.3 copy-done
  535.6 89.9 %all-gather.22.cloned.1.call-done = bf16[2048,2048]{1,0:T(8,128)(2,1)} async-done(((bf16[1024,2048]{1,0:T(8,128)(2,1)}), bf16[2048,2048]{1,0:T(8,128)(2,1)}) %all-gather.22.cloned.1.call-update) | async-done | bytes 8388624 | tf_op jit(solution)/shard_map/all_gather | solution.py:142
  625.5 14.6 fusion.51
  640.0 91.0 %all-gather.24.cloned.1.call-done = bf16[2048,2048]{1,0:T(8,128)(2,1)} async-done(((bf16[1024,2048]{1,0:T(8,128)(2,1)}), bf16[2048,2048]{1,0:T(8,128)(2,1)}) %all-gather.24.cloned.1.call-update) | async-done | bytes 8388624 | tf_op jit(solution)/shard_map/all_gather | solution.py:143
  731.0 14.5 fusion.52
  745.5 90.9 %all-gather.26.cloned.1.call-done = bf16[2048,2048]{1,0:T(8,128)(2,1)} async-done(((bf16[2048,1024]{1,0:T(8,128)(2,1)}), bf16[2048,2048]{1,0:T(8,128)(2,1)}) %all-gather.26.cloned.1.call-update) | async-done | bytes 8388624 | tf_op jit(solution)/shard_map/all_gather | solution.py:144
  836.4 21.9 multiply_convert_fusion
  858.3 12.7 fusion.54
  871.1 12.7 fusion.53
  883.8 13.3 convolution_add_fusion
  897.2 562.3 %all-reduce.12.cloned.1.call-done = (f32[1024,2048]{1,0:T(8,128)}, f32[1024,2048]{1,0:T(8,128)}) async-done(((f32[1024,2048]{1,0:T(8,128)}, f32[1024,2048]{1,0:T(8,128)}), (f32[1024,2048]{1,0:T(8,128)}, f32[1024,2048]{1,0:T(8,128)})) %all-reduce.12.cloned.1.call-update) | async-done | bytes 16777232 | tf_op jit(solution)/shard_map/psum | solution.py:155
  1459.6 15.1 multiply_reduce_fusion
  1474.6 4.7 subtract_add_fusion
  1479.4 3.2 copy-done.1
  1482.6 4.0 fusion.23
  1489.3 9.5 select_convert_fusion
  1498.8 6.3 broadcast_multiply_fusion
  1505.2 13.1 fusion.17
  1518.3 9.0 copy.61
  1527.4 7.7 multiply_bitcast_fusion
  1535.1 40.4 %reduce-scatter.10.cloned.1.call-done = f32[4,256,512]{1,2,0:T(8,128)} async-done(((f32[4,1024,512]{1,2,0:T(8,128)}), f32[4,256,512]{1,2,0:T(8,128)}) %reduce-scatter.10.cloned.1.call-update) | async-done | bytes 2097168 | tf_op jit(solution)/shard_map/reduce_scatter | solution.py:217
  1580.6 68.9 %reduce-scatter.12.cloned.1.call-done = f32[4,256,512]{2,1,0:T(8,128)} async-done(((f32[4,1024,512]{2,1,0:T(8,128)}), f32[4,256,512]{2,1,0:T(8,128)}) %reduce-scatter.12.cloned.1.call-update) | async-done | bytes 2097168 | tf_op jit(solution)/shard_map/reduce_scatter | solution.py:218
  1651.3 4.3 fusion.30
  1658.0 5.8 add_add_fusion
  1665.1 7.7 fusion.19
  1672.9 15.6 fusion.55
  1688.5 15.4 fusion.56
  1704.0 15.6 fusion.57
  1719.7 6.6 convolution_bitcast_fusion
  1726.4 6.6 fusion.32
  1733.1 6.5 fusion.28
  1741.0 213.9 %all-reduce.10.cloned.1.call-done = f32[1024,2048]{1,0:T(8,128)} async-done(((f32[1024,2048]{1,0:T(8,128)}), f32[1024,2048]{1,0:T(8,128)}) %all-reduce.10.cloned.1.call-update) | async-done | bytes 8388624 | tf_op jit(solution)/shard_map/psum | solution.py:231
  1954.9 6.4 fusion.3
  1961.3 25.5 %all-reduce.2 = (f32[2048]{0:T(1024)S(1)}, f32[2048]{0:T(1024)S(1)}, f32[]{:T(128)}, f32[]{:T(128)}, f32[]{:T(128)}) all-reduce(f32[2048]{0:T(1024)S(1)} %get-tuple-element.16, f32[2048]{0:T(1024)S(1)} %copy-done.27, f32[]{:T(128)} %get-tuple-element.19, ...), channel_id=4, replica_groups=mesh['fsdp'=2,'ctx'=4,'tp'=4] {'fsdp','ctx'}, use_global_device_ids=true, to_apply=%region_11.12.clone | all-reduce | flops 4099 | bytes 32792
  1990.2 10.5 fusion.10
  2000.6 8.1 reduce-scatter.20.cloned.1.call-done
  2008.8 120.2 %reduce-scatter.22.cloned.1.call-done = f32[256,2048]{1,0:T(8,128)} async-done(((f32[2048,2048]{1,0:T(8,128)}), f32[256,2048]{1,0:T(8,128)}) %reduce-scatter.22.cloned.1.call-update) | async-done | bytes 2097168 | tf_op jit(solution)/shard_map/reduce_scatter | solution.py:249
  2129.0 120.2 %reduce-scatter.24.cloned.1.call-done = f32[256,2048]{1,0:T(8,128)} async-done(((f32[2048,2048]{1,0:T(8,128)}), f32[256,2048]{1,0:T(8,128)}) %reduce-scatter.24.cloned.1.call-update) | async-done | bytes 2097168 | tf_op jit(solution)/shard_map/reduce_scatter | solution.py:250
  2249.2 120.0 %reduce-scatter.26.cloned.1.call-done = f32[2048,256]{1,0:T(8,128)} async-done(((f32[2048,2048]{1,0:T(8,128)}), f32[2048,256]{1,0:T(8,128)}) %reduce-scatter.26.cloned.1.call-update) | async-done | bytes 2097168 | tf_op jit(solution)/shard_map/reduce_scatter | solution.py:251
  2369.2 55.1 %reduce-scatter.18.cloned.1.call-done = f32[256,512]{1,0:T(8,128)} async-done(((f32[2048,512]{1,0:T(8,128)}), f32[256,512]{1,0:T(8,128)}) %reduce-scatter.18.cloned.1.call-update) | async-done | bytes 524304 | tf_op jit(solution)/shard_map/reduce_scatter | solution.py:246
  2424.3 55.0 %reduce-scatter.14.cloned.1.call-done = f32[256,512]{1,0:T(8,128)} async-done(((f32[2048,512]{1,0:T(8,128)}), f32[256,512]{1,0:T(8,128)}) %reduce-scatter.14.cloned.1.call-update) | async-done | bytes 524304 | tf_op jit(solution)/shard_map/reduce_scatter | solution.py:244
  2479.3 55.1 %reduce-scatter.16.cloned.1.call-done = f32[256,512]{1,0:T(8,128)} async-done(((f32[2048,512]{1,0:T(8,128)}), f32[256,512]{1,0:T(8,128)}) %reduce-scatter.16.cloned.1.call-update) | async-done | bytes 524304 | tf_op jit(solution)/shard_map/reduce_scatter | solution.py:245
  (136 shorter events, 30.7 us)
Async XLA Ops:
  7.2 38.2 %all-gather.16.cloned.1.call-start = ((), (), s32[]{:S(2)}) async-start(), calls=%async_computation.12 | async-start | bytes 3145728 | tf_op jit(solution)/shard_map/all_gather | solution.py:92
  7.9 72.1 %all-gather.14.cloned.1.call-start = ((), (), s32[]{:S(2)}) async-start(), calls=%async_computation.11 | async-start | bytes 3145728 | tf_op jit(solution)/shard_map/all_gather | solution.py:91
  8.7 106.1 %all-gather.10.cloned.1.call-start = ((), (), s32[]{:S(2)}) async-start(), calls=%async_computation.9 | async-start | bytes 3145728 | tf_op jit(solution)/shard_map/all_gather | solution.py:93
  9.4 142.3 %all-gather.18.cloned.1.call-start = ((), (), s32[]{:S(2)}) async-start(), calls=%async_computation.13 | async-start | bytes 5242880 | tf_op jit(solution)/shard_map/all_gather | solution.py:129
  14.9 78.2 %copy-start.23 = (f32[2048]{0:T(1024)}, f32[2048]{0:T(1024)S(1)}, u32[]{:S(2)}) copy-start(f32[2048]{0:T(1024)S(1)} %convert_element_type.133) | copy-start | bytes 24580
  25.4 65.7 %copy-start.10 = (f32[4,256,64]{1,2,0:T(8,128)}, f32[4,256,64]{1,2,0:T(8,128)S(1)}, u32[]{:S(2)}) copy-start(f32[4,256,64]{1,2,0:T(8,128)S(1)} %get-tuple-element.48) | copy-start | bytes 786436
  25.4 65.7 %copy-start.12 = (f32[4,256,64]{1,2,0:T(8,128)}, f32[4,256,64]{1,2,0:T(8,128)S(1)}, u32[]{:S(2)}) copy-start(f32[4,256,64]{1,2,0:T(8,128)S(1)} %get-tuple-element.49) | copy-start | bytes 786436
  84.0 4.7 copy-start.7
  84.0 4.7 copy-start.16
  91.8 59.9 %copy-start.17 = (bf16[4,256,4,64]{1,3,2,0:T(8,128)(2,1)}, bf16[4,256,4,64]{1,3,2,0:T(8,128)(2,1)S(1)}, u32[]{:S(2)}) copy-start(bf16[4,256,4,64]{1,3,2,0:T(8,128)(2,1)S(1)} %get-tuple-element.40) | copy-start | bytes 1572868
  91.8 59.9 %copy-start.19 = (bf16[4,256,4,64]{1,3,2,0:T(8,128)(2,1)}, bf16[4,256,4,64]{1,3,2,0:T(8,128)(2,1)S(1)}, u32[]{:S(2)}) copy-start(bf16[4,256,4,64]{1,3,2,0:T(8,128)(2,1)S(1)} %get-tuple-element.41) | copy-start | bytes 1572868
  93.0 95.2 %all-gather.12.cloned.1.call-start = ((), (), s32[]{:S(2)}) async-start(), calls=%async_computation.10 | async-start | bytes 5242880 | tf_op jit(solution)/shard_map/all_gather | solution.py:130
  93.1 27.8 %copy-start.25 = (f32[1,2,4,128]{3,1,2,0:T(2,128)}, f32[1,2,4,128]{3,1,2,0:T(2,128)S(1)}, u32[]{:S(2)}) copy-start(f32[1,2,4,128]{3,1,2,0:T(2,128)S(1)} %copy.68) | copy-start | bytes 12292
  98.3 23.2 copy-start.28
  120.9 101.8 %all-gather.20.cloned.1.call-start = ((), (), s32[]{:S(2)}) async-start(), calls=%async_computation.14 | async-start | bytes 3145728 | tf_op jit(solution)/shard_map/all_gather | solution.py:94
  121.5 399.4 %all-reduce.8.cloned.1.call-start = ((), (), s32[]{:S(2)}) async-start(), calls=%async_computation.15 | async-start | bytes 16777216 | tf_op jit(solution)/shard_map/psum | solution.py:139
  127.6 66.8 %copy-start.4 = (pred[4,256,1024]{2,1,0:T(8,128)(4,1)}, pred[4,256,1024]{2,1,0:T(8,128)(4,1)S(1)}, u32[]{:S(2)}) copy-start(pred[4,256,1024]{2,1,0:T(8,128)(4,1)S(1)} %broadcast_compare_fusion) | copy-start | bytes 3145732
  206.1 23.8 copy-start.8
  230.0 2.1 copy-start.29
  230.0 395.5 %all-gather.22.cloned.1.call-start = ((), (), s32[]{:S(2)}) async-start(), calls=%async_computation.16 | async-start | bytes 12582912 | tf_op jit(solution)/shard_map/all_gather | solution.py:142
  230.7 500.3 %all-gather.24.cloned.1.call-start = ((), (), s32[]{:S(2)}) async-start(), calls=%async_computation.17 | async-start | bytes 12582912 | tf_op jit(solution)/shard_map/all_gather | solution.py:143
  231.5 605.0 %all-gather.26.cloned.1.call-start = ((), (), s32[]{:S(2)}) async-start(), calls=%async_computation.18 | async-start | bytes 12582912 | tf_op jit(solution)/shard_map/all_gather | solution.py:144
  232.0 1227.5 %all-reduce.12.cloned.1.call-start = ((), (), s32[]{:S(2)}) async-start(), calls=%async_computation.29 | async-start | bytes 33554432 | tf_op jit(solution)/shard_map/psum | solution.py:155
  528.5 4.3 copy-start
  858.3 12.7 copy-start.30
  871.1 12.7 copy-start.32
  897.2 678.3 %reduce-scatter.10.cloned.1.call-start = ((), (), s32[]{:S(2)}) async-start(), calls=%async_computation.19 | async-start | bytes 10485760 | tf_op jit(solution)/shard_map/reduce_scatter | solution.py:217
  1459.5 15.1 copy-start.3
  1459.6 15.1 copy-start.6
  1479.4 3.3 copy-start.1
  1482.6 6.7 copy-start.5
  1489.3 9.5 copy-start.18
  1498.8 6.3 copy-start.2
  1505.2 144.3 %reduce-scatter.12.cloned.1.call-start = ((), (), s32[]{:S(2)}) async-start(), calls=%async_computation.20 | async-start | bytes 10485760 | tf_op jit(solution)/shard_map/reduce_scatter | solution.py:218
  1527.3 48.2 %copy-start.11 = (f32[4,256,64]{1,2,0:T(8,128)S(1)}, f32[4,256,64]{1,2,0:T(8,128)}, u32[]{:S(2)}) copy-start(f32[4,256,64]{1,2,0:T(8,128)} %copy-done.10) | copy-start | bytes 786436
  1527.3 48.2 %copy-start.13 = (f32[4,256,64]{1,2,0:T(8,128)S(1)}, f32[4,256,64]{1,2,0:T(8,128)}, u32[]{:S(2)}) copy-start(f32[4,256,64]{1,2,0:T(8,128)} %copy-done.12) | copy-start | bytes 786436
  1527.3 427.5 %all-reduce.10.cloned.1.call-start = ((), (), s32[]{:S(2)}) async-start(), calls=%async_computation.21 | async-start | bytes 16777216 | tf_op jit(solution)/shard_map/psum | solution.py:231
  1579.3 76.4 %copy-start.15 = (bf16[2048,512]{1,0:T(8,128)(2,1)S(1)}, bf16[2048,512]{1,0:T(8,128)(2,1)}, u32[]{:S(2)}) copy-start(bf16[2048,512]{1,0:T(8,128)(2,1)} %all-gather.14.cloned.1.call-done) | copy-start | bytes 6291460
  1649.5 6.1 copy-start.21
  1655.6 2.4 copy-start.14
  1663.9 1.2 copy-start.9
  1663.9 344.9 %reduce-scatter.20.cloned.1.call-start = ((), (), s32[]{:S(2)}) async-start(), calls=%async_computation.25 | async-start | bytes 4718592 | tf_op jit(solution)/shard_map/reduce_scatter | solution.py:247
  1672.9 456.1 %reduce-scatter.22.cloned.1.call-start = ((), (), s32[]{:S(2)}) async-start(), calls=%async_computation.26 | async-start | bytes 18874368 | tf_op jit(solution)/shard_map/reduce_scatter | solution.py:249
  1688.5 560.7 %reduce-scatter.24.cloned.1.call-start = ((), (), s32[]{:S(2)}) async-start(), calls=%async_computation.27 | async-start | bytes 18874368 | tf_op jit(solution)/shard_map/reduce_scatter | solution.py:250
  1703.9 665.3 %reduce-scatter.26.cloned.1.call-start = ((), (), s32[]{:S(2)}) async-start(), calls=%async_computation.28 | async-start | bytes 18874368 | tf_op jit(solution)/shard_map/reduce_scatter | solution.py:251
  1719.6 6.8 copy-start.22
  1719.6 704.7 %reduce-scatter.18.cloned.1.call-start = ((), (), s32[]{:S(2)}) async-start(), calls=%async_computation.24 | async-start | bytes 4718592 | tf_op jit(solution)/shard_map/reduce_scatter | solution.py:246
  1726.3 753.0 %reduce-scatter.14.cloned.1.call-start = ((), (), s32[]{:S(2)}) async-start(), calls=%async_computation.22 | async-start | bytes 4718592 | tf_op jit(solution)/shard_map/reduce_scatter | solution.py:244
  1726.4 6.7 copy-start.20
  1733.0 6.7 copy-start.31
  1733.1 7.9 copy-start.26
  1733.1 221.8 %copy-start.24 = (f32[2048]{0:T(1024)S(1)}, f32[2048]{0:T(1024)}, u32[]{:S(2)}) copy-start(f32[2048]{0:T(1024)} %copy-done.23) | copy-start | bytes 24580
  1733.1 801.4 %reduce-scatter.16.cloned.1.call-start = ((), (), s32[]{:S(2)}) async-start(), calls=%async_computation.23 | async-start | bytes 4718592 | tf_op jit(solution)/shard_map/reduce_scatter | solution.py:245
  1739.7 221.6 %copy-start.27 = (f32[2048]{0:T(1024)S(1)}, f32[2048]{0:T(1024)}, u32[]{:S(2)}) copy-start(f32[2048]{0:T(1024)} %get-tuple-element.21) | copy-start | bytes 24580
Sparse Core Ops, SparseCore 0:
  9.5 35.8 all-gather.15
  46.9 33.0 all-gather.13
  81.6 33.0 all-gather.9
  116.7 34.9 all-gather.17
  153.7 34.4 all-gather.11
  189.6 33.0 all-gather.19
  230.1 290.8 all-reduce.7
  522.5 102.9 all-gather.21
  627.0 103.9 all-gather.23
  732.4 103.9 all-gather.25
  897.3 562.2 all-reduce.11
  1505.3 70.1 reduce-scatter.9
  1578.1 71.3 reduce-scatter.11
  1664.0 290.8 all-reduce.9
  1958.6 50.0 reduce-scatter.19
  2012.7 116.1 reduce-scatter.21
  2133.0 116.1 reduce-scatter.23
  2253.2 115.9 reduce-scatter.25
  2373.1 51.1 reduce-scatter.17
  2428.1 51.1 reduce-scatter.13
  2483.3 51.1 reduce-scatter.15
where the time goes:
time: 2550 us
  waiting for transfers between devices  2110 us (83%)
  matrix products  260 us (10%)
  other arithmetic  69.3 us (3%)
  blocking collectives  41.2 us (2%)
  local copies, waits for them, and re-layouts  38.8 us (2%)
    psum x1, waiting for transfers between devices, local(): feed_out = lax.psum(plain_dot(hidden, down_full), 'tp')  562 us
    psum x1, waiting for transfers between devices, local(): attend_out = lax.psum(plain_dot(mixed_rows, output_full), 'tp')  284 us
    psum x1, waiting for transfers between devices, local(): lax.psum(dot_last(grad_query_rows, query_full) + dot_last(grad_key_rows,...  214 us
    reduce_scatter x1, waiting for transfers between devices, local(): lax.psum_scatter(grad_gate_w, ('fsdp', 'ctx'), scatter_dimension=0, tiled...  120 us
    reduce_scatter x1, waiting for transfers between devices, local(): lax.psum_scatter(grad_up_w, ('fsdp', 'ctx'), scatter_dimension=0, tiled=T...  120 us
    reduce_scatter x1, waiting for transfers between devices, local(): lax.psum_scatter(grad_down, ('fsdp', 'ctx'), scatter_dimension=1, tiled=T...  120 us
    all_gather x1, waiting for transfers between devices, local(): lax.all_gather(w_up, 'fsdp', axis=0, tiled=True)  91 us
    all_gather x1, waiting for transfers between devices, local(): lax.all_gather(w_down, 'fsdp', axis=1, tiled=True)  90.9 us
  transfers between devices with their start and end apart: 21, of which 21 were waited for; matrix products, arithmetic and copies ran while one was open for 9% of the time, Pallas kernels for 0%

commit v1 on v0

v1 whole, which is shorter than its diff:
```python
import math

import jax
import jax.numpy as jnp
from jax import lax
from jax.sharding import PartitionSpec as P

HD = 128


norm_epsilon = 1e-05
rope_base = 10000.0


def plain_dot(left_side, right_side):
    return jnp.dot(left_side, right_side, preferred_element_type=jnp.float32)


def dot_last(left_side, right_side):
    return lax.dot_general(
        left_side, right_side, (((1,), (1,)), ((), ())), preferred_element_type=jnp.float32
    )


def dot_first(left_side, right_side):
    return lax.dot_general(
        left_side, right_side, (((0,), (0,)), ((), ())), preferred_element_type=jnp.float32
    )


def inverse_rms(values):
    return lax.rsqrt(jnp.mean(values * values, axis=-1, keepdims=True) + norm_epsilon)


def norm_back(grad_norm, values, scale_rows, gain):
    weighted = grad_norm * gain
    inner_mean = jnp.mean(weighted * values, axis=-1, keepdims=True)
    grad_values = (
        scale_rows * weighted - values * (scale_rows * scale_rows * scale_rows) * inner_mean
    )
    grad_gain = jnp.sum(grad_norm * (values * scale_rows), axis=0)
    return (grad_values, grad_gain)


def rope_tables(positions, head_size):
    half_size = head_size // 2
    inverse = jnp.exp(
        jnp.arange(half_size, dtype=jnp.float32) * (-2.0 * math.log(rope_base) / head_size)
    )
    turned = positions.astype(jnp.float32)[..., None, None] * inverse
    return (jnp.cos(turned), jnp.sin(turned))


def rotate(values, cosine, sine_table, direction):
    half_size = values.shape[-1] // 2
    first_half = values[..., :half_size]
    second_half = values[..., half_size:]
    return jnp.concatenate(
        [
            first_half * cosine - direction * (second_half * sine_table),
            direction * (first_half * sine_table) + second_half * cosine,
        ],
        axis=-1,
    )


def spread_rows(piece, ctx_size):
    part = piece.shape[0] // ctx_size
    mine = lax.dynamic_slice_in_dim(piece, lax.axis_index("ctx") * part, part, 0)
    return lax.all_gather(mine, ("fsdp", "ctx"), axis=0, tiled=True)


def spread_columns(piece, ctx_size):
    part = piece.shape[0] // ctx_size
    mine = lax.dynamic_slice_in_dim(piece, lax.axis_index("ctx") * part, part, 0)
    held = lax.all_gather(mine, ("fsdp", "ctx"), axis=0, tiled=True)
    fsdp_size = lax.axis_size("fsdp")
    held = held.reshape(fsdp_size, piece.shape[0], piece.shape[1])
    return jnp.swapaxes(held, 0, 1).reshape(piece.shape[0], fsdp_size * piece.shape[1])


def sum_rows(partial):
    return lax.psum_scatter(
        partial.astype(jnp.bfloat16), "tp", scatter_dimension=0, tiled=True
    ).astype(jnp.float32)


def every_row(rows):
    return lax.all_gather(rows, "tp", axis=0, tiled=True)


def local(
    tokens,
    positions,
    block_ids,
    gain_attend,
    w_query,
    w_key,
    w_value,
    w_output,
    gain_feed,
    w_gate,
    w_up,
    w_down,
    cotangent,
):
    seq_count, block_len, model_width = tokens.shape
    row_count = seq_count * block_len
    ctx_size = lax.axis_size("ctx")
    tp_size = lax.axis_size("tp")
    seq_len = block_len * ctx_size
    heads_here = w_query.shape[1] // HD
    width_here = heads_here * HD
    score_scale = 1.0 / math.sqrt(HD)
    score_shift = math.log(seq_len)
    shape_heads = (seq_count, block_len, heads_here, HD)
    low = jnp.bfloat16
    part_rows = row_count // tp_size
    row_at = lax.axis_index("tp") * part_rows

    token_rows = tokens.reshape(row_count, model_width)
    grad_rows = cotangent.reshape(row_count, model_width)
    token_part = lax.dynamic_slice_in_dim(token_rows, row_at, part_rows, 0).astype(jnp.float32)
    cotangent_part = lax.dynamic_slice_in_dim(grad_rows, row_at, part_rows, 0).astype(jnp.float32)

    qkv_full = spread_rows(jnp.concatenate([w_query, w_key, w_value], axis=1), ctx_size)
    gains = lax.all_gather(jnp.stack([gain_attend, gain_feed]), "fsdp", axis=1, tiled=True)
    gain_one = gains[0].astype(jnp.float32)
    gain_two = gains[1].astype(jnp.float32)
    output_full = spread_columns(w_output, ctx_size)
    gate_full = spread_rows(w_gate, ctx_size)
    up_full = spread_rows(w_up, ctx_size)
    down_full = spread_columns(w_down, ctx_size)

    stream = token_rows.astype(jnp.float32)
    scale_one = inverse_rms(stream)
    normed_one = (stream * scale_one * gain_one).astype(low)
    projected = plain_dot(normed_one, qkv_full)
    queries = projected[:, :width_here]
    key_proj = projected[:, width_here : 2 * width_here]
    values = projected[:, 2 * width_here :].astype(low)
    cosine, sine_table = rope_tables(positions, HD)
    query_rot = rotate(queries.reshape(shape_heads), cosine, sine_table, 1.0).astype(low)
    key_rot = rotate(key_proj.reshape(shape_heads), cosine, sine_table, 1.0).astype(low)

    key_value = lax.all_gather(
        jnp.concatenate(
            [
                key_rot.reshape(seq_count, block_len, width_here),
                values.reshape(seq_count, block_len, width_here),
            ],
            axis=2,
        ),
        "ctx",
        axis=1,
        tiled=True,
    )
    key_tags = lax.all_gather(block_ids, "ctx", axis=1, tiled=True)
    key_heads = key_value[:, :, :width_here].reshape(seq_count, seq_len, heads_here, HD)
    value_heads = key_value[:, :, width_here:].reshape(seq_count, seq_len, heads_here, HD)
    logits = (
        jnp.einsum("sqhd,skhd->shqk", query_rot, key_heads, preferred_element_type=jnp.float32)
        * score_scale
        - score_shift
    )
    allowed = key_tags[:, None, None, :] <= block_ids[:, None, :, None]
    squashed = jax.nn.sigmoid(logits)
    weights = jnp.where(allowed, squashed, 0.0).astype(low)
    attended = jnp.einsum(
        "shqk,skhd->sqhd", weights, value_heads, preferred_element_type=jnp.float32
    )
    mixed_rows = attended.reshape(row_count, width_here).astype(low)

    attend_part = sum_rows(plain_dot(mixed_rows, output_full))
    middle = token_part + attend_part
    scale_two = inverse_rms(middle)
    normed_two = every_row((middle * scale_two * gain_two).astype(low))

    gate_vals = plain_dot(normed_two, gate_full)
    up_vals = plain_dot(normed_two, up_full)
    gate_sig = jax.nn.sigmoid(gate_vals)
    gate_act = gate_vals * gate_sig
    hidden = (gate_act * up_vals).astype(low)
    grad_hidden = dot_last(grad_rows, down_full)
    slope = gate_sig * (1.0 + gate_vals * (1.0 - gate_sig))
    grad_gate = (grad_hidden * up_vals * slope).astype(low)
    grad_up = (grad_hidden * gate_act).astype(low)
    grad_normed_two = sum_rows(dot_last(grad_gate, gate_full) + dot_last(grad_up, up_full))

    feed_part = sum_rows(plain_dot(hidden, down_full))
    result = middle + feed_part
    layer_out = every_row(result.astype(low)).reshape(tokens.shape)

    grad_middle_norm, grad_gain_two = norm_back(grad_normed_two, middle, scale_two, gain_two)
    grad_middle = cotangent_part + grad_middle_norm
    grad_attend = every_row(grad_middle.astype(low))

    def scatter(value, dimension):
        return lax.psum_scatter(
            value.astype(low), ("fsdp", "ctx"), scatter_dimension=dimension, tiled=True
        ).astype(jnp.float32)

    grad_down = scatter(dot_first(hidden, grad_rows), 1)
    grad_gate_w = scatter(dot_first(normed_two, grad_gate), 0)
    grad_up_w = scatter(dot_first(normed_two, grad_up), 0)

    grad_mixed = dot_last(grad_attend, output_full).astype(low)
    grad_output_w = scatter(dot_first(mixed_rows, grad_attend), 1)
    grad_mixed_heads = grad_mixed.reshape(shape_heads)
    grad_weights = jnp.einsum(
        "sqhd,skhd->shqk", grad_mixed_heads, value_heads, preferred_element_type=jnp.float32
    )
    grad_logits = jnp.where(allowed, grad_weights * squashed * (1.0 - squashed), 0.0).astype(low)
    grad_query = score_scale * jnp.einsum(
        "shqk,skhd->sqhd", grad_logits, key_heads, preferred_element_type=jnp.float32
    )
    key_part = score_scale * jnp.einsum(
        "shqk,sqhd->skhd", grad_logits, query_rot, preferred_element_type=jnp.float32
    )
    value_part = jnp.einsum(
        "shqk,sqhd->skhd", weights, grad_mixed_heads, preferred_element_type=jnp.float32
    )
    pair = jnp.concatenate(
        [
            key_part.reshape(seq_count, seq_len, width_here).astype(low),
            value_part.reshape(seq_count, seq_len, width_here).astype(low),
        ],
        axis=2,
    )
    mine = lax.psum_scatter(pair, "ctx", scatter_dimension=1, tiled=True).astype(jnp.float32)
    grad_query_rows = rotate(grad_query, cosine, sine_table, -1.0).reshape(row_count, width_here)
    grad_key_rows = rotate(
        mine[:, :, :width_here].reshape(shape_heads), cosine, sine_table, -1.0
    ).reshape(row_count, width_here)
    grad_qkv = jnp.concatenate(
        [
            grad_query_rows.astype(low),
            grad_key_rows.astype(low),
            mine[:, :, width_here:].reshape(row_count, width_here).astype(low),
        ],
        axis=1,
    )
    grad_normed_one = sum_rows(dot_last(grad_qkv, qkv_full))
    grad_qkv_w = scatter(dot_first(normed_one, grad_qkv), 0)
    scale_one_part = lax.dynamic_slice_in_dim(scale_one, row_at, part_rows, 0)
    grad_input_norm, grad_gain_one = norm_back(
        grad_normed_one, token_part, scale_one_part, gain_one
    )
    grad_input = every_row((grad_middle + grad_input_norm).astype(low)).reshape(tokens.shape)

    sums = jnp.stack(
        [jnp.sum(result * result), jnp.sum(attend_part * attend_part), jnp.sum(feed_part * feed_part)]
    )
    small = lax.psum(
        jnp.concatenate([grad_gain_one, grad_gain_two, sums]), ("fsdp", "ctx", "tp")
    )
    shards = lax.axis_size("fsdp") * ctx_size
    entries = float(row_count * model_width * shards)
    roots = jnp.sqrt(small[2 * model_width :] / entries)
    gain_part = model_width // shards
    gain_at = (lax.axis_index("fsdp") * ctx_size + lax.axis_index("ctx")) * gain_part
    grad_gain_attend = lax.dynamic_slice_in_dim(small, gain_at, gain_part, 0)
    grad_gain_feed = lax.dynamic_slice_in_dim(small, model_width + gain_at, gain_part, 0)
    return (
        layer_out,
        grad_input,
        grad_gain_attend,
        grad_qkv_w[:, :width_here],
        grad_qkv_w[:, width_here : 2 * width_here],
        grad_qkv_w[:, 2 * width_here :],
        grad_output_w,
        grad_gain_feed,
        grad_gate_w,
        grad_up_w,
        grad_down,
        roots[0],
        roots[1],
        roots[2],
    )


def solution(mesh):
    placed = (
        P("fsdp", "ctx", None),
        P("fsdp", "ctx"),
        P("fsdp", "ctx"),
        P("fsdp"),
        P("fsdp", "tp"),
        P("fsdp", "tp"),
        P("fsdp", "tp"),
        P("tp", "fsdp"),
        P("fsdp"),
        P("fsdp", "tp"),
        P("fsdp", "tp"),
        P("tp", "fsdp"),
        P("fsdp", "ctx", None),
    )
    return jax.shard_map(
        local,
        mesh=mesh,
        in_specs=placed,
        out_specs=(
            P("fsdp", "ctx", None),
            P("fsdp", "ctx", None),
            P(("fsdp", "ctx")),
            P(("fsdp", "ctx"), "tp"),
            P(("fsdp", "ctx"), "tp"),
            P(("fsdp", "ctx"), "tp"),
            P("tp", ("fsdp", "ctx")),
            P(("fsdp", "ctx")),
            P(("fsdp", "ctx"), "tp"),
            P(("fsdp", "ctx"), "tp"),
            P("tp", ("fsdp", "ctx")),
            P(),
            P(),
            P(),
        ),
        check_vma=False,
    )
```

time: 2550 us -> 1560 us (0.61)
  waiting for transfers between devices: 2110 us -> 1110 us
  local copies, waits for them, and re-layouts: 38.8 us -> 81.4 us
  matrix products: 260 us -> 233 us
    psum x3 -> x0, waiting for transfers between devices: 1060 us -> none  [the longest x1 562 us: local(): feed_out = lax.psum(plain_dot(hidden, down_full), 'tp')]
    all_gather x9 -> x10, waiting for transfers between devices: 406 us -> 546 us  [the longest x4 324 us: every_row(): return lax.all_gather(rows, 'tp', axis=0, tiled=True)]
    reduce_scatter x9 -> x10, waiting for transfers between devices: 643 us -> 567 us  [the longest x5 277 us: scatter(): lax.psum_scatter(value.astype(low), ('fsdp', 'ctx'), scatter_dimension=di...]
    psum x0 -> x1, blocking collectives: none -> 40 us  [local(): lax.psum(jnp.concatenate([grad_gain_one, grad_gain_two, sums]), ('fsdp',...]
    unnamed x1 -> x0, blocking collectives: 25.5 us -> none
    dot_general x7 -> x5, matrix products: 74.1 us -> 59.5 us  [dot_first(): lax.dot_general(left_side, right_side, (((0,), (0,)), ((), ())), preferre...]
    dot_general x7 -> x5, matrix products: 64.5 us -> 59.2 us  [dot_last(): lax.dot_general(left_side, right_side, (((1,), (1,)), ((), ())), preferre...]
    dot_general x7 -> x5, matrix products: 62.2 us -> 59.6 us  [plain_dot(): return jnp.dot(left_side, right_side, preferred_element_type=jnp.float32)]
  transfers between devices with their start and end apart: 21 -> 20, of which waited for: 21 -> 19; matrix products, arithmetic and copies ran while one was open for 9% -> 12% of each run, Pallas kernels for 0% -> 0%
where the time goes in v1:
time: 1560 us; the launch traced here: 1550 us
  waiting for transfers between devices  1110 us (71%)
  matrix products  233 us (15%)
  local copies, waits for them, and re-layouts  81.4 us (5%)
  other arithmetic  55.9 us (4%)
  blocking collectives  50.7 us (3%)
    all_gather x4, waiting for transfers between devices, every_row(): return lax.all_gather(rows, 'tp', axis=0, tiled=True)  324 us
    reduce_scatter x5, waiting for transfers between devices, scatter(): lax.psum_scatter(value.astype(low), ('fsdp', 'ctx'), scatter_dimension=di...  277 us
    reduce_scatter x4, waiting for transfers between devices, sum_rows(): lax.psum_scatter(partial.astype(jnp.bfloat16), 'tp', scatter_dimension=0,...  229 us
    all_gather x3, waiting for transfers between devices, spread_rows(): return lax.all_gather(mine, ('fsdp', 'ctx'), axis=0, tiled=True)  122 us
    reduce_scatter x1, waiting for transfers between devices, local(): lax.psum_scatter(pair, 'ctx', scatter_dimension=1, tiled=True)  61.7 us
    dot_general x5, matrix products, plain_dot(): return jnp.dot(left_side, right_side, preferred_element_type=jnp.float32)  59.6 us
    dot_general x5, matrix products, dot_first(): lax.dot_general(left_side, right_side, (((0,), (0,)), ((), ())), preferre...  59.5 us
    dot_general x5, matrix products, dot_last(): lax.dot_general(left_side, right_side, (((1,), (1,)), ((), ())), preferre...  59.2 us
  transfers between devices with their start and end apart: 20, of which 19 were waited for; matrix products, arithmetic and copies ran while one was open for 12% of the time, Pallas kernels for 0%

profile of v1, /device:TPU:0, one launch (start us, length us, event | category | flops | bytes accessed | tf_op | source)
XLA Modules:
  0.0 1552.7 jit_solution(17306718815725621846)
XLA Ops:
  10.4 5.3 all_gather.36
  15.7 3.1 multiply_reduce_fusion
  21.3 37.3 %all-gather.11.cloned.1.call-done = bf16[2048,1536]{1,0:T(8,128)(2,1)} async-done(((bf16[256,1536]{1,0:T(8,128)(2,1)}), bf16[2048,1536]{1,0:T(8,128)(2,1)}) %all-gather.11.cloned.1.call-update) | async-done | bytes 6291472 | tf_op jit(solution)/shard_map/all_gather | solution.py:70
  58.7 10.1 fusion.23
  76.5 2.9 reshape.171
  79.4 4.6 fusion.43
  84.1 2.7 subtract_convert_fusion.2
  89.5 5.4 all_gather.39
  95.7 4.0 copy.66
  99.7 50.8 %all-gather.13.cloned.1.call-done = bf16[4,1024,1024]{1,2,0:T(8,128)(2,1)} async-done(((bf16[4,256,1024]{1,2,0:T(8,128)(2,1)}), bf16[4,1024,1024]{1,2,0:T(8,128)(2,1)}) %all-gather.13.cloned.1.call-update) | async-done | bytes 8388624 | tf_op jit(solution)/shard_map/all_gather | solution.py:146
  150.5 5.3 fusion.40
  155.8 8.5 add_divide_fusion
  164.3 10.0 fusion.21
  175.7 6.3 convolution_convert_fusion.6
  186.8 72.2 %reduce-scatter.11.cloned.1.call-done = bf16[256,2048]{1,0:T(8,128)(2,1)} async-done(((bf16[1024,2048]{1,0:T(8,128)(2,1)}), bf16[256,2048]{1,0:T(8,128)(2,1)}) %reduce-scatter.11.cloned.1.call-update) | async-done | bytes 1048592 | tf_op jit(solution)/shard_map/reduce_scatter | solution.py:83
  261.0 2.9 multiply_convert_fusion.3
  266.7 48.8 %all-gather.23.cloned.1.call-done = bf16[4096,1024]{1,0:T(8,128)(2,1)} async-done(((bf16[512,1024]{1,0:T(8,128)(2,1)}), bf16[4096,1024]{1,0:T(8,128)(2,1)}) %all-gather.23.cloned.1.call-update) | async-done | bytes 8388624 | tf_op jit(solution)/shard_map/all_gather | solution.py:76
  315.5 11.9 copy.67
  327.4 44.1 %all-gather.21.cloned.1.call-done = bf16[2048,2048]{1,0:T(8,128)(2,1)} async-done(((bf16[256,2048]{1,0:T(8,128)(2,1)}), bf16[2048,2048]{1,0:T(8,128)(2,1)}) %all-gather.21.cloned.1.call-update) | async-done | bytes 8388624 | tf_op jit(solution)/shard_map/all_gather | solution.py:70
  371.6 82.9 %all-gather.17.cloned.1.call-done = bf16[1024,2048]{1,0:T(8,128)(2,1)} async-done(((bf16[256,2048]{1,0:T(8,128)(2,1)}), bf16[1024,2048]{1,0:T(8,128)(2,1)}) %all-gather.17.cloned.1.call-update) | async-done | bytes 4194320 | tf_op jit(solution)/shard_map/all_gather | solution.py:89
  454.5 14.6 fusion.50
  469.0 40.7 %all-gather.19.cloned.1.call-done = bf16[2048,2048]{1,0:T(8,128)(2,1)} async-done(((bf16[256,2048]{1,0:T(8,128)(2,1)}), bf16[2048,2048]{1,0:T(8,128)(2,1)}) %all-gather.19.cloned.1.call-update) | async-done | bytes 8388624 | tf_op jit(solution)/shard_map/all_gather | solution.py:70
  509.7 14.7 fusion.49
  524.4 19.1 %fusion.2 = (bf16[1024,2048]{1,0:T(8,128)(2,1)}, bf16[1024,2048]{1,0:T(8,128)(2,1)}, bf16[1024,2048]{1,0:T(8,128)(2,1)}) fusion(f32[1024,2048]{1,0:T(8,128)} %fusion.49, f32[1024,2048]{1,0:T(8,128)} %fusion.50, bf16[1024,2048]{1,0:T(8,128)(2,1)S(1)} %bitcast.143, bf16[2048,2048]{0,1:T(8,128)(2,1)} %bitcast.121), kind=kOutput, calls=%fused_computation.8 | convolution fusion | flops 8621391872 | bytes 41943040 | tf_op jit(solution)/shard_map/dot_general | solution.py:20
  543.5 12.9 fusion.51
  556.4 12.9 add_convert_fusion
  569.3 14.0 convolution_convert_fusion.5
  583.6 62.6 %reduce-scatter.15.cloned.1.call-done = bf16[256,2048]{1,0:T(8,128)(2,1)} async-done(((bf16[1024,2048]{1,0:T(8,128)(2,1)}), bf16[256,2048]{1,0:T(8,128)(2,1)}) %reduce-scatter.15.cloned.1.call-update) | async-done | bytes 1048592 | tf_op jit(solution)/shard_map/reduce_scatter | solution.py:83
  646.2 79.4 %reduce-scatter.13.cloned.1.call-done = bf16[256,2048]{1,0:T(8,128)(2,1)} async-done(((bf16[1024,2048]{1,0:T(8,128)(2,1)}), bf16[256,2048]{1,0:T(8,128)(2,1)}) %reduce-scatter.13.cloned.1.call-update) | async-done | bytes 1048592 | tf_op jit(solution)/shard_map/reduce_scatter | solution.py:83
  725.7 5.1 fusion.16
  730.8 3.4 fusion.39
  734.2 81.4 %all-gather.27.cloned.1.call-done = bf16[1024,2048]{1,0:T(8,128)(2,1)} async-done(((bf16[256,2048]{1,0:T(8,128)(2,1)}), bf16[1024,2048]{1,0:T(8,128)(2,1)}) %all-gather.27.cloned.1.call-update) | async-done | bytes 4194320 | tf_op jit(solution)/shard_map/all_gather | solution.py:89
  815.6 6.2 convolution_convert_fusion.9
  826.2 9.5 select_convert_fusion
  835.7 12.9 convolution_convert_fusion.8
  848.6 5.9 multiply_convert_fusion
  854.4 7.7 pad_maximum_fusion
  862.7 7.7 multiply_bitcast_fusion
  870.4 61.7 %reduce-scatter.17.cloned.1.call-done = bf16[4,256,1024]{1,2,0:T(8,128)(2,1)} async-done(((bf16[4,1024,1024]{1,2,0:T(8,128)(2,1)}), bf16[4,256,1024]{1,2,0:T(8,128)(2,1)}) %reduce-scatter.17.cloned.1.call-update) | async-done | bytes 2097168 | tf_op jit(solution)/shard_map/reduce_scatter | solution.py:230
  932.1 3.0 fusion.42
  937.4 2.8 fusion.45
  940.2 3.2 copy.88
  943.3 3.2 copy.89
  946.5 3.5 subtract_convert_fusion.1
  954.2 8.2 convolution_convert_fusion.4
  962.7 14.1 convolution_convert_fusion
  976.9 14.2 convolution_convert_fusion.1
  991.4 14.0 convolution_convert_fusion.2
  1006.6 5.9 convolution_convert_fusion.7
  1012.6 11.2 convolution_convert_fusion.3
  1024.5 14.9 reduce-scatter.19.cloned.1.call-done
  1042.0 4.3 fusion.10
  1046.4 68.2 %reduce-scatter.29.cloned.1.call-done = bf16[2048,256]{1,0:T(8,128)(2,1)} async-done(((bf16[2048,2048]{1,0:T(8,128)(2,1)}), bf16[2048,256]{1,0:T(8,128)(2,1)}) %reduce-scatter.29.cloned.1.call-update) | async-done | bytes 1048592 | tf_op jit(solution)/shard_map/reduce_scatter | solution.py:199
  1114.6 2.7 convert_element_type.201
  1117.3 72.1 %reduce-scatter.27.cloned.1.call-done = bf16[256,2048]{1,0:T(8,128)(2,1)} async-done(((bf16[2048,2048]{1,0:T(8,128)(2,1)}), bf16[256,2048]{1,0:T(8,128)(2,1)}) %reduce-scatter.27.cloned.1.call-update) | async-done | bytes 1048592 | tf_op jit(solution)/shard_map/reduce_scatter | solution.py:199
  1189.4 2.8 convert_element_type.199
  1192.2 72.0 %reduce-scatter.25.cloned.1.call-done = bf16[256,2048]{1,0:T(8,128)(2,1)} async-done(((bf16[2048,2048]{1,0:T(8,128)(2,1)}), bf16[256,2048]{1,0:T(8,128)(2,1)}) %reduce-scatter.25.cloned.1.call-update) | async-done | bytes 1048592 | tf_op jit(solution)/shard_map/reduce_scatter | solution.py:199
  1264.3 2.8 convert_element_type.197
  1267.1 79.4 %all-gather.25.cloned.1.call-done = bf16[1024,2048]{1,0:T(8,128)(2,1)} async-done(((bf16[256,2048]{1,0:T(8,128)(2,1)}), bf16[1024,2048]{1,0:T(8,128)(2,1)}) %all-gather.25.cloned.1.call-update) | async-done | bytes 4194320 | tf_op jit(solution)/shard_map/all_gather | solution.py:89
  1346.5 43.4 %reduce-scatter.23.cloned.1.call-done = bf16[512,256]{1,0:T(8,128)(2,1)} async-done(((bf16[512,2048]{1,0:T(8,128)(2,1)}), bf16[512,256]{1,0:T(8,128)(2,1)}) %reduce-scatter.23.cloned.1.call-update) | async-done | bytes 262160 | tf_op jit(solution)/shard_map/reduce_scatter | solution.py:199
  1393.6 40.0 %psum.7 = f32[4099]{0:T(1024)S(1)} all-reduce(f32[4099]{0:T(1024)S(1)} %concatenate.39), channel_id=1, replica_groups=mesh['fsdp'=2,'ctx'=4,'tp'=4] {'fsdp','ctx','tp'}, use_global_device_ids=true, to_apply=%region_14.15 | all-reduce | flops 4099 | bytes 32792 | tf_op jit(solution)/shard_map/psum | solution.py:254
  1434.8 20.8 %reduce-scatter.21.cloned.1.call-done = bf16[256,1536]{1,0:T(8,128)(2,1)} async-done(((bf16[2048,1536]{1,0:T(8,128)(2,1)}), bf16[256,1536]{1,0:T(8,128)(2,1)}) %reduce-scatter.21.cloned.1.call-update) | async-done | bytes 786448 | tf_op jit(solution)/shard_map/reduce_scatter | solution.py:199
  1458.0 80.4 %all-gather.29.cloned.1.call-done = bf16[1024,2048]{1,0:T(8,128)(2,1)} async-done(((bf16[256,2048]{1,0:T(8,128)(2,1)}), bf16[1024,2048]{1,0:T(8,128)(2,1)}) %all-gather.29.cloned.1.call-update) | async-done | bytes 4194320 | tf_op jit(solution)/shard_map/all_gather | solution.py:89
  1538.5 4.9 copy.117
  (148 shorter events, 53.8 us)
Async XLA Ops:
  7.2 2.3 copy-start
  7.2 3.1 copy-start.22
  7.2 3.1 copy-start.25
  7.2 3.1 copy-start.26
  7.2 51.4 %all-gather.11.cloned.1.call-start = ((), (), s32[]{:S(2)}) async-start(), calls=%async_computation.10 | async-start | bytes 7077888 | tf_op jit(solution)/shard_map/all_gather | solution.py:70
  9.4 86.2 %all-gather.15.cloned.1.call-start = ((), (), s32[]{:S(2)}) async-start(), calls=%async_computation.12 | async-start | bytes 2359296 | tf_op jit(solution)/shard_map/all_gather | solution.py:76
  10.2 140.2 %all-gather.13.cloned.1.call-start = ((), (), s32[]{:S(2)}) async-start(), calls=%async_computation.11 | async-start | bytes 10485760 | tf_op jit(solution)/shard_map/all_gather | solution.py:146
  19.4 49.4 %copy-start.23 = (f32[1,2,4,128]{3,1,2,0:T(2,128)}, f32[1,2,4,128]{3,1,2,0:T(2,128)S(1)}, u32[]{:S(2)}) copy-start(f32[1,2,4,128]{3,1,2,0:T(2,128)S(1)} %copy.90) | copy-start | bytes 12292
  19.4 49.4 %copy-start.18 = (f32[1,2048]{1,0:T(1,128)}, f32[1,2048]{1,0:T(1,128)S(1)}, u32[]{:S(2)}) copy-start(f32[1,2048]{1,0:T(1,128)S(1)} %get-tuple-element.57) | copy-start | bytes 24580
  21.3 62.8 %copy-start.7 = (f32[4,256,64]{2,1,0:T(8,128)}, f32[4,256,64]{2,1,0:T(8,128)S(1)}, u32[]{:S(2)}) copy-start(f32[4,256,64]{2,1,0:T(8,128)S(1)} %get-tuple-element.58) | copy-start | bytes 786436
  21.3 62.8 %copy-start.8 = (f32[4,256,64]{2,1,0:T(8,128)}, f32[4,256,64]{2,1,0:T(8,128)S(1)}, u32[]{:S(2)}) copy-start(f32[4,256,64]{2,1,0:T(8,128)S(1)} %get-tuple-element.59) | copy-start | bytes 786436
  86.8 1.2 copy-start.12
  87.4 2.2 copy-start.20
  89.5 169.5 %reduce-scatter.11.cloned.1.call-start = ((), (), s32[]{:S(2)}) async-start(), calls=%async_computation.13 | async-start | bytes 5242880 | tf_op jit(solution)/shard_map/reduce_scatter | solution.py:83
  99.6 56.1 %copy-start.9 = (bf16[4,256,4,64]{3,1,2,0:T(8,128)(2,1)S(1)}, bf16[4,256,4,64]{3,1,2,0:T(8,128)(2,1)}, u32[]{:S(2)}) copy-start(bf16[4,256,4,64]{3,1,2,0:T(8,128)(2,1)} %get-tuple-element.32) | copy-start | bytes 1572868
  150.5 5.3 copy-start.10
  155.8 8.5 copy-start.4
  182.0 133.5 %all-gather.23.cloned.1.call-start = ((), (), s32[]{:S(2)}) async-start(), calls=%async_computation.17 | async-start | bytes 9437184 | tf_op jit(solution)/shard_map/all_gather | solution.py:76
  184.4 187.2 %all-gather.21.cloned.1.call-start = ((), (), s32[]{:S(2)}) async-start(), calls=%async_computation.16 | async-start | bytes 9437184 | tf_op jit(solution)/shard_map/all_gather | solution.py:70
  186.8 267.7 %all-gather.17.cloned.1.call-start = ((), (), s32[]{:S(2)}) async-start(), calls=%async_computation.14 | async-start | bytes 5242880 | tf_op jit(solution)/shard_map/all_gather | solution.py:89
  263.9 245.8 %all-gather.19.cloned.1.call-start = ((), (), s32[]{:S(2)}) async-start(), calls=%async_computation.15 | async-start | bytes 9437184 | tf_op jit(solution)/shard_map/all_gather | solution.py:70
  266.3 379.9 %reduce-scatter.15.cloned.1.call-start = ((), (), s32[]{:S(2)}) async-start(), calls=%async_computation.20 | async-start | bytes 5242880 | tf_op jit(solution)/shard_map/reduce_scatter | solution.py:83
  509.7 14.7 copy-start.17
  543.5 12.9 copy-start.27
  569.3 156.4 %reduce-scatter.13.cloned.1.call-start = ((), (), s32[]{:S(2)}) async-start(), calls=%async_computation.18 | async-start | bytes 5242880 | tf_op jit(solution)/shard_map/reduce_scatter | solution.py:83
  583.3 142.4 %copy-start.3 = (bf16[256,2048]{1,0:T(8,128)(2,1)S(1)}, bf16[256,2048]{1,0:T(8,128)(2,1)}, u32[]{:S(2)}) copy-start(bf16[256,2048]{1,0:T(8,128)(2,1)} %reduce-scatter.11.cloned.1.call-done) | copy-start | bytes 3145732
  583.3 232.3 %all-gather.27.cloned.1.call-start = ((), (), s32[]{:S(2)}) async-start(), calls=%async_computation.21 | async-start | bytes 5242880 | tf_op jit(solution)/shard_map/all_gather | solution.py:89
  725.7 5.1 copy-start.5
  734.2 197.9 %reduce-scatter.17.cloned.1.call-start = ((), (), s32[]{:S(2)}) async-start(), calls=%async_computation.22 | async-start | bytes 10485760 | tf_op jit(solution)/shard_map/reduce_scatter | solution.py:230
  835.6 12.9 copy-start.2
  862.2 177.2 %reduce-scatter.19.cloned.1.call-start = ((), (), s32[]{:S(2)}) async-start(), calls=%async_computation.23 | async-start | bytes 5242880 | tf_op jit(solution)/shard_map/reduce_scatter | solution.py:83
  946.5 7.8 slice-start
  950.0 4.2 slice-start.1
  951.6 1.6 copy-start.15
  951.6 2.6 copy-start.14
  953.2 1.0 copy-start.16
  962.5 152.1 %reduce-scatter.29.cloned.1.call-start = ((), (), s32[]{:S(2)}) async-start(), calls=%async_computation.29 | async-start | bytes 9437184 | tf_op jit(solution)/shard_map/reduce_scatter | solution.py:199
  976.8 212.6 %reduce-scatter.27.cloned.1.call-start = ((), (), s32[]{:S(2)}) async-start(), calls=%async_computation.28 | async-start | bytes 9437184 | tf_op jit(solution)/shard_map/reduce_scatter | solution.py:199
  991.1 273.2 %reduce-scatter.25.cloned.1.call-start = ((), (), s32[]{:S(2)}) async-start(), calls=%async_computation.27 | async-start | bytes 9437184 | tf_op jit(solution)/shard_map/reduce_scatter | solution.py:199
  1005.4 1.2 copy-start.13
  1005.4 341.0 %all-gather.25.cloned.1.call-start = ((), (), s32[]{:S(2)}) async-start(), calls=%async_computation.19 | async-start | bytes 5242880 | tf_op jit(solution)/shard_map/all_gather | solution.py:89
  1006.0 6.6 copy-start.19
  1006.0 6.6 copy-start.24
  1006.0 383.8 %reduce-scatter.23.cloned.1.call-start = ((), (), s32[]{:S(2)}) async-start(), calls=%async_computation.26 | async-start | bytes 2359296 | tf_op jit(solution)/shard_map/reduce_scatter | solution.py:199
  1012.5 443.1 %reduce-scatter.21.cloned.1.call-start = ((), (), s32[]{:S(2)}) async-start(), calls=%async_computation.25 | async-start | bytes 7077888 | tf_op jit(solution)/shard_map/reduce_scatter | solution.py:199
  1023.9 0.7 copy-start.21
  1023.9 18.2 %copy-start.6 = (bf16[256,2048]{1,0:T(8,128)(2,1)S(1)}, bf16[256,2048]{1,0:T(8,128)(2,1)}, u32[]{:S(2)}) copy-start(bf16[256,2048]{1,0:T(8,128)(2,1)} %reduce-scatter.15.cloned.1.call-done) | copy-start | bytes 3145732
  1023.9 514.6 %all-gather.29.cloned.1.call-start = ((), (), s32[]{:S(2)}) async-start(), calls=%async_computation.24 | async-start | bytes 5242880 | tf_op jit(solution)/shard_map/all_gather | solution.py:89
  1538.4 4.9 copy-start.11
  1538.5 7.0 copy-start.1
Sparse Core Ops, SparseCore 0:
  10.5 48.1 all-gather.10
  61.1 27.7 all-gather.14
  91.1 59.3 all-gather.12
  182.2 76.7 reduce-scatter.10
  260.7 54.7 all-gather.22
  317.3 54.2 all-gather.20
  373.7 80.7 all-gather.16
  456.9 52.7 all-gather.18
  569.4 76.7 reduce-scatter.14
  648.3 77.2 reduce-scatter.12
  734.3 81.2 all-gather.26
  862.3 69.7 reduce-scatter.16
  962.6 76.7 reduce-scatter.18
  1042.8 71.7 reduce-scatter.28
  1117.9 71.4 reduce-scatter.26
  1192.7 71.4 reduce-scatter.24
  1265.7 80.7 all-gather.24
  1350.2 39.6 reduce-scatter.22
  1393.2 62.4 reduce-scatter.20
  1457.7 80.7 all-gather.28

commit v2 on v1

--- a/solution.py
+++ b/solution.py
@@ -3,6 +3,8 @@
 import jax
 import jax.numpy as jnp
 from jax import lax
+from jax.experimental import pallas as pl
+from jax.experimental.pallas import tpu as pltpu
 from jax.sharding import PartitionSpec as P
 
 HD = 128
@@ -79,14 +81,736 @@
     return jnp.swapaxes(held, 0, 1).reshape(piece.shape[0], fsdp_size * piece.shape[1])
 
 
-def sum_rows(partial):
-    return lax.psum_scatter(
-        partial.astype(jnp.bfloat16), "tp", scatter_dimension=0, tiled=True
-    ).astype(jnp.float32)
-
-
-def every_row(rows):
-    return lax.all_gather(rows, "tp", axis=0, tiled=True)
+CHUNK = 32
+GROUP = 4
+TILE = 512
+VMEM_BYTES = 66000000
+MESH_ID = pl.DeviceIdType.MESH
+
+
+def chunk_rows(index, rows=CHUNK):
+    return pl.ds(pl.multiple_of(index * rows, rows), rows)
+
+
+def fold_rows(values):
+    return jnp.sum(values.reshape(values.shape[0] // 8, 8, values.shape[1]), axis=0)
+
+
+class Line:
+    def __init__(self, size, chunks, own, held, out, sems):
+        self.size, self.chunks, self.own, self.held, self.out, self.sems = (
+            size,
+            chunks,
+            own,
+            held,
+            out,
+            sems,
+        )
+        self.rank = lax.axis_index("tp")
+        self.is_end = (self.rank == 0) | (self.rank == size - 1)
+        self.end_half = jnp.where(self.rank == 0, 0, 1)
+
+    def enter(self):
+        barrier = pltpu.get_barrier_semaphore()
+        rank, size = self.rank, self.size
+
+        @pl.when(rank > 0)
+        def _():
+            pl.semaphore_signal(
+                barrier, inc=1, device_id={"tp": rank - 1}, device_id_type=MESH_ID
+            )
+
+        @pl.when(rank < size - 1)
+        def _():
+            pl.semaphore_signal(
+                barrier, inc=1, device_id={"tp": rank + 1}, device_id_type=MESH_ID
+            )
+
+        pl.semaphore_wait(barrier, jnp.where(self.is_end, 1, 2))
+
+    def place(self, half):
+        rank, size = self.rank, self.size
+        if half == 0:
+            return size - 1 - rank, jnp.maximum(rank - 1, 0), jnp.minimum(rank + 1, size - 1)
+        return rank, jnp.minimum(rank + 1, size - 1), jnp.maximum(rank - 1, 0)
+
+    def send_on(self, half, chunk, target, first):
+        rows = chunk_rows(chunk)
+        source = self.own if first else self.held
+        return pltpu.make_async_remote_copy(
+            src_ref=source.at[half, rows],
+            dst_ref=self.held.at[half, rows],
+            send_sem=self.sems.at[0, half, chunk],
+            recv_sem=self.sems.at[1, half, chunk],
+            device_id={"tp": target},
+            device_id_type=MESH_ID,
+        )
+
+    def send_back(self, half, chunk, target):
+        rows = chunk_rows(chunk)
+        return pltpu.make_async_remote_copy(
+            src_ref=self.out.at[half, rows],
+            dst_ref=self.out.at[half, rows],
+            send_sem=self.sems.at[2, half, chunk],
+            recv_sem=self.sems.at[3, half, chunk],
+            device_id={"tp": target},
+            device_id_type=MESH_ID,
+        )
+
+    def slot(self, step, finish, arrived):
+        last = self.size - 1
+        for half in (0, 1):
+            place, onward, back = self.place(half)
+            chunk = step - place
+            rows = chunk_rows(chunk)
+
+            @pl.when((chunk >= 0) & (chunk < self.chunks) & (place == 0))
+            def _():
+                self.send_on(half, chunk, onward, True).start()
+
+            @pl.when((chunk >= 0) & (chunk < self.chunks) & (place > 0) & (place < last))
+            def _():
+                self.send_on(half, chunk, onward, False).wait_recv()
+                total = self.held[half, rows].astype(jnp.float32) + self.own[half, rows].astype(
+                    jnp.float32
+                )
+                self.held[half, rows] = total.astype(jnp.bfloat16)
+                self.send_on(half, chunk, onward, False).start()
+
+            @pl.when((chunk >= 0) & (chunk < self.chunks) & (place == last))
+            def _():
+                self.send_on(half, chunk, onward, False).wait_recv()
+
+        chunk = step - last
+        rows = chunk_rows(chunk)
+
+        @pl.when((chunk >= 0) & (chunk < self.chunks) & self.is_end)
+        def _():
+            half = self.end_half
+            total = self.held[half, rows].astype(jnp.float32) + self.own[half, rows].astype(
+                jnp.float32
+            )
+            finish(chunk, total)
+            inward = jnp.where(self.rank == 0, 1, last - 1)
+            self.send_back(half, chunk, inward).start()
+            arrived(half, chunk)
+
+        for half in (0, 1):
+            place, onward, back = self.place(half)
+            chunk = step - last - (last - place)
+
+            @pl.when((chunk >= 0) & (chunk < self.chunks) & (place < last))
+            def _():
+                self.send_back(half, chunk, back).wait_recv()
+
+                @pl.when(place > 0)
+                def _():
+                    self.send_back(half, chunk, back).start()
+
+                arrived(half, chunk)
+
+    def leave(self):
+        last = self.size - 1
+
+        @pl.loop(0, self.chunks)
+        def _(chunk):
+            for half in (0, 1):
+                place, onward, back = self.place(half)
+
+                @pl.when(place < last)
+                def _():
+                    self.send_on(half, chunk, onward, True).wait_send()
+
+                @pl.when(place > 0)
+                def _():
+                    self.send_back(half, chunk, back).wait_send()
+
+
+def load_all(pairs, sems):
+    return [
+        pltpu.make_async_copy(source, target, sems.at[index])
+        for index, (source, target) in enumerate(pairs)
+    ]
+
+
+def feed_kernel(
+    size,
+    partial,
+    tokens,
+    cotangent,
+    gate,
+    up,
+    down,
+    gain,
+    normed_out,
+    hidden_out,
+    grad_gate_out,
+    grad_up_out,
+    middle_out,
+    square_out,
+    own,
+    held,
+    out,
+    stream,
+    cot,
+    gate_in,
+    up_in,
+    down_in,
+    middle,
+    staged,
+    sems,
+    load_sems,
+    save_sems,
+    stage_sems,
+    middle_sem,
+):
+    half_rows = own.shape[1]
+    chunks = half_rows // CHUNK
+    width = gate_in.shape[1]
+    tiles = width // TILE
+    group_rows = GROUP * CHUNK
+    groups = chunks // GROUP
+    line = Line(size, chunks, own, held, out, sems)
+    half = line.end_half
+    loads = load_all(
+        [
+            (partial, own),
+            (tokens.at[half], stream),
+            (cotangent, cot),
+            (gate, gate_in),
+            (up, up_in),
+            (down, down_in),
+        ],
+        load_sems,
+    )
+    for load in loads:
+        load.start()
+    square_out[...] = jnp.zeros_like(square_out)
+    line.enter()
+    loads[0].wait()
+    loads[1].wait()
+
+    def finish(chunk, total):
+        rows = chunk_rows(chunk)
+        mid = stream[rows].astype(jnp.float32) + total
+        square_out[...] += fold_rows(total * total)
+        middle[rows] = mid
+        out[half, rows] = (mid * inverse_rms(mid) * gain[...]).astype(jnp.bfloat16)
+
+    def save(which, chunk):
+        rows = chunk_rows(chunk)
+        return pltpu.make_async_copy(
+            out.at[which, rows], normed_out.at[which, rows], save_sems.at[which, chunk]
+        )
+
+    def arrived(which, chunk):
+        save(which, chunk).start()
+
+    def stage(index, which, slot, group, tile):
+        target = (hidden_out, grad_gate_out, grad_up_out)[index]
+        return pltpu.make_async_copy(
+            staged.at[slot, index, which],
+            target.at[which, chunk_rows(group, group_rows), chunk_rows(tile, TILE)],
+            stage_sems.at[slot, index, which],
+        )
+
+    head = 2 * (size - 1) + GROUP - 1
+    units = groups * tiles
+
+    @pl.loop(0, head + max(chunks, units) + 1)
+    def _(step):
+        line.slot(step, finish, arrived)
+        unit = step - head
+
+        @pl.when(unit == 0)
+        def _():
+            for load in loads[2:]:
+                load.wait()
+
+        @pl.when((unit >= 0) & (unit < units))
+        def _():
+            group = unit // tiles
+            tile = unit % tiles
+            slot = unit % 2
+            group_at = chunk_rows(group, group_rows)
+            tile_at = chunk_rows(tile, TILE)
+
+            @pl.when(unit >= 2)
+            def _():
+                for index in range(3):
+                    for which in (0, 1):
+                        stage(index, which, slot, group, tile).wait()
+
+            rows = out[:, group_at].reshape(2 * group_rows, out.shape[2])
+            outer = cot[:, group_at].reshape(2 * group_rows, out.shape[2])
+            gate_vals = plain_dot(rows, gate_in[:, tile_at])
+            up_vals = plain_dot(rows, up_in[:, tile_at])
+            grad_hidden = dot_last(outer, down_in[tile_at])
+            gate_sig = jax.nn.sigmoid(gate_vals)
+            gate_act = gate_vals * gate_sig
+            slope = gate_sig * (1.0 + gate_vals * (1.0 - gate_sig))
+            made = (gate_act * up_vals, grad_hidden * up_vals * slope, grad_hidden * gate_act)
+            for index in range(3):
+                staged[slot, index] = (
+                    made[index].astype(jnp.bfloat16).reshape(2, group_rows, TILE)
+                )
+                for which in (0, 1):
+                    stage(index, which, slot, group, tile).start()
+
+    @pl.when(line.is_end)
+    def _():
+        pltpu.make_async_copy(middle, middle_out, middle_sem).start()
+
+    @pl.loop(0, chunks)
+    def _(chunk):
+        for which in (0, 1):
+            save(which, chunk).wait()
+
+    for slot in (0, 1):
+        for index in range(3):
+            for which in (0, 1):
+                stage(index, which, slot, 0, 0).wait()
+    line.leave()
+
+    @pl.when(line.is_end)
+    def _():
+        pltpu.make_async_copy(middle, middle_out, middle_sem).wait()
+
+
+def feed_block(partial, tokens, cotangent, gate, up, down, gain, size):
+    rows, model_width = partial.shape
+    half_rows = rows // 2
+    width = gate.shape[1]
+    low = jnp.bfloat16
+    chunks = half_rows // CHUNK
+    anywhere = pl.BlockSpec(memory_space=pl.ANY)
+    local_spec = pl.BlockSpec(memory_space=pltpu.VMEM)
+    halves = (2, half_rows, model_width)
+    hidden_shape = jax.ShapeDtypeStruct((2, half_rows, width), low)
+    outs = pl.pallas_call(
+        lambda *refs: feed_kernel(size, *refs),
+        out_shape=(
+            jax.ShapeDtypeStruct(halves, low),
+            hidden_shape,
+            hidden_shape,
+            hidden_shape,
+            jax.ShapeDtypeStruct((half_rows, model_width), jnp.float32),
+            jax.ShapeDtypeStruct((8, model_width), jnp.float32),
+        ),
+        in_specs=[anywhere] * 6 + [local_spec],
+        out_specs=[anywhere] * 5 + [local_spec],
+        scratch_shapes=[
+            pltpu.VMEM(halves, low),
+            pltpu.VMEM(halves, low),
+            pltpu.VMEM(halves, low),
+            pltpu.VMEM((half_rows, model_width), low),
+            pltpu.VMEM(halves, low),
+            pltpu.VMEM(gate.shape, low),
+            pltpu.VMEM(up.shape, low),
+            pltpu.VMEM(down.shape, low),
+            pltpu.VMEM((half_rows, model_width), jnp.float32),
+            pltpu.VMEM((2, 3, 2, GROUP * CHUNK, TILE), low),
+            pltpu.SemaphoreType.DMA((4, 2, chunks)),
+            pltpu.SemaphoreType.DMA((6,)),
+            pltpu.SemaphoreType.DMA((2, chunks)),
+            pltpu.SemaphoreType.DMA((2, 3, 2)),
+            pltpu.SemaphoreType.DMA(()),
+        ],
+        compiler_params=pltpu.CompilerParams(
+            collective_id=1, has_side_effects=True, vmem_limit_bytes=VMEM_BYTES
+        ),
+        cost_estimate=pl.CostEstimate(
+            flops=6 * rows * model_width * width, bytes_accessed=300000000, transcendentals=0
+        ),
+        name="feed_block",
+    )(
+        partial.reshape(halves),
+        tokens.reshape(halves),
+        cotangent.reshape(halves),
+        gate,
+        up,
+        down,
+        gain.reshape(1, model_width),
+    )
+    normed, hidden, grad_gate, grad_up, middle, squares = outs
+    flat = (rows, width)
+    return (
+        normed.reshape(rows, model_width),
+        hidden.reshape(flat),
+        grad_gate.reshape(flat),
+        grad_up.reshape(flat),
+        middle,
+        squares,
+    )
+
+
+def back_kernel(
+    size,
+    hidden,
+    grad_gate,
+    grad_up,
+    gate,
+    up,
+    down,
+    cotangent,
+    middle,
+    gain,
+    attend_out,
+    layer_out,
+    grad_middle_out,
+    sum_out,
+    own,
+    held,
+    out,
+    gate_in,
+    up_in,
+    down_in,
+    left,
+    cot,
+    mid,
+    grad_mid,
+    sems,
+    load_sems,
+    left_sems,
+    end_sems,
+    save_sems,
+):
+    half_rows = hidden.shape[1]
+    chunks = half_rows // CHUNK
+    model_width = gate_in.shape[0]
+    tiles = model_width // TILE
+    group_rows = GROUP * CHUNK
+    groups = chunks // GROUP
+    last = size - 1
+    line = Line(size, 2 * chunks, own, held, out, sems)
+    half = line.end_half
+    loads = load_all([(gate, gate_in), (up, up_in), (down, down_in)], load_sems)
+    for load in loads:
+        load.start()
+
+    def fetch(source, group, slot, place):
+        rows = chunk_rows(lax.rem(group, groups), group_rows)
+        return pltpu.make_async_copy(
+            source.at[:, rows], left.at[slot, place], left_sems.at[slot, place]
+        )
+
+    def start_fetch(group):
+        slot = lax.rem(group, 2)
+
+        @pl.when(group < groups)
+        def _():
+            fetch(grad_gate, group, slot, 0).start()
+            fetch(grad_up, group, slot, 1).start()
+
+        @pl.when((group >= groups) & (group < 2 * groups))
+        def _():
+            fetch(hidden, group, slot, 0).start()
+
+    def make(group, tile):
+        slot = lax.rem(group, 2)
+        tile_at = chunk_rows(tile, TILE)
+        rows_at = chunk_rows(group, group_rows)
+
+        @pl.when(tile == 0)
+        def _():
+            @pl.when(group < groups)
+            def _():
+                fetch(grad_gate, group, slot, 0).wait()
+                fetch(grad_up, group, slot, 1).wait()
+
+            @pl.when(group >= groups)
+            def _():
+                fetch(hidden, group, slot, 0).wait()
+
+            start_fetch(group + 1)
+
+        shape = (2 * group_rows, left.shape[4])
+
+        @pl.when(group < groups)
+        def _():
+            total = dot_last(left[slot, 0].reshape(shape), gate_in[tile_at]) + dot_last(
+                left[slot, 1].reshape(shape), up_in[tile_at]
+            )
+            own[:, rows_at, tile_at] = total.astype(jnp.bfloat16).reshape(2, group_rows, TILE)
+
+        @pl.when(group >= groups)
+        def _():
+            total = plain_dot(left[slot, 0].reshape(shape), down_in[:, tile_at])
+            own[:, rows_at, tile_at] = total.astype(jnp.bfloat16).reshape(2, group_rows, TILE)
+
+    def fetch_end(chunk, slot):
+        rows = chunk_rows(lax.rem(chunk, chunks))
+        return (
+            pltpu.make_async_copy(middle.at[rows], mid.at[slot], end_sems.at[slot, 0]),
+            pltpu.make_async_copy(cotangent.at[half, rows], cot.at[slot], end_sems.at[slot, 1]),
+        )
+
+    def grad_save(chunk, slot):
+        return pltpu.make_async_copy(
+            grad_mid.at[slot], grad_middle_out.at[chunk_rows(chunk)], end_sems.at[slot, 2]
+        )
+
+    start_fetch(0)
+    sum_out[...] = jnp.zeros_like(sum_out)
+    line.enter()
+    loads[0].wait()
+    loads[1].wait()
+
+    @pl.when(line.is_end)
+    def _():
+        for copy in fetch_end(0, 0):
+            copy.start()
+
+    @pl.loop(0, tiles)
+    def _(tile):
+        make(0, tile)
+
+    loads[2].wait()
+
+    def finish(chunk, total):
+        slot = lax.rem(chunk, 2)
+        for copy in fetch_end(chunk, slot):
+            copy.wait()
+
+        @pl.when(chunk + 1 < 2 * chunks)
+        def _():
+            for copy in fetch_end(chunk + 1, 1 - slot):
+                copy.start()
+
+        mids = mid[slot]
+        rows = chunk_rows(chunk)
+
+        @pl.when(chunk < chunks)
+        def _():
+            scale = inverse_rms(mids)
+            weighted = total * gain[...]
+            inner = jnp.mean(weighted * mids, axis=-1, keepdims=True)
+            grad = (
+                cot[slot].astype(jnp.float32)
+                + scale * weighted
+                - mids * (scale * scale * scale * inner)
+            )
+            sum_out[0] += fold_rows(total * (mids * scale))
+            out[half, rows] = grad.astype(jnp.bfloat16)
+
+            @pl.when(chunk >= 2)
+            def _():
+                grad_save(chunk - 2, slot).wait()
+
+            grad_mid[slot] = grad
+            grad_save(chunk, slot).start()
+
+        @pl.when(chunk >= chunks)
+        def _():
+            result = mids + total
+            sum_out[1] += fold_rows(result * result)
+            sum_out[2] += fold_rows(total * total)
+            out[half, rows] = result.astype(jnp.bfloat16)
+
+    def save(which, chunk, target):
+        rows = chunk_rows(lax.rem(chunk, chunks))
+        return pltpu.make_async_copy(
+            out.at[which, chunk_rows(chunk)],
+            target.at[which, rows],
+            save_sems.at[which, chunk],
+        )
+
+    def arrived(which, chunk):
+        @pl.when(chunk < chunks)
+        def _():
+            save(which, chunk, attend_out).start()
+
+        @pl.when(chunk >= chunks)
+        def _():
+            save(which, chunk, layer_out).start()
+
+    @pl.loop(0, 2 * chunks + 2 * last)
+    def _(step):
+        line.slot(step, finish, arrived)
+        unit = step + tiles
+
+        @pl.when(unit < 2 * groups * tiles)
+        def _():
+            make(unit // tiles, unit % tiles)
+
+    @pl.loop(0, chunks)
+    def _(chunk):
+        for which in (0, 1):
+            save(which, chunk, attend_out).wait()
+            save(which, chunk + chunks, layer_out).wait()
+
+    @pl.when(line.is_end)
+    def _():
+        for chunk in (chunks - 2, chunks - 1):
+            grad_save(chunk, chunk % 2).wait()
+
+    line.leave()
+
+
+def back_block(hidden, grad_gate, grad_up, gate, up, down, cotangent, middle, gain, size):
+    rows, width = hidden.shape
+    model_width = gate.shape[0]
+    half_rows = rows // 2
+    low = jnp.bfloat16
+    chunks = half_rows // CHUNK
+    anywhere = pl.BlockSpec(memory_space=pl.ANY)
+    local_spec = pl.BlockSpec(memory_space=pltpu.VMEM)
+    halves = (2, half_rows, model_width)
+    hidden_halves = (2, half_rows, width)
+    both = (2, 2 * half_rows, model_width)
+    grad_attend, layer, grad_middle, sums = pl.pallas_call(
+        lambda *refs: back_kernel(size, *refs),
+        out_shape=(
+            jax.ShapeDtypeStruct(halves, low),
+            jax.ShapeDtypeStruct(halves, low),
+            jax.ShapeDtypeStruct((half_rows, model_width), jnp.float32),
+            jax.ShapeDtypeStruct((3, 8, model_width), jnp.float32),
+        ),
+        in_specs=[anywhere] * 8 + [local_spec],
+        out_specs=[anywhere] * 3 + [local_spec],
+        scratch_shapes=[
+            pltpu.VMEM(both, low),
+            pltpu.VMEM(both, low),
+            pltpu.VMEM(both, low),
+            pltpu.VMEM(gate.shape, low),
+            pltpu.VMEM(up.shape, low),
+            pltpu.VMEM(down.shape, low),
+            pltpu.VMEM((2, 2, 2, GROUP * CHUNK, width), low),
+            pltpu.VMEM((2, CHUNK, model_width), low),
+            pltpu.VMEM((2, CHUNK, model_width), jnp.float32),
+            pltpu.VMEM((2, CHUNK, model_width), jnp.float32),
+            pltpu.SemaphoreType.DMA((4, 2, 2 * chunks)),
+            pltpu.SemaphoreType.DMA((3,)),
+            pltpu.SemaphoreType.DMA((2, 2)),
+            pltpu.SemaphoreType.DMA((2, 3)),
+            pltpu.SemaphoreType.DMA((2, 2 * chunks)),
+        ],
+        compiler_params=pltpu.CompilerParams(
+            collective_id=2, has_side_effects=True, vmem_limit_bytes=VMEM_BYTES
+        ),
+        cost_estimate=pl.CostEstimate(
+            flops=6 * rows * model_width * width, bytes_accessed=600000000, transcendentals=0
+        ),
+        name="back_block",
+    )(
+        hidden.reshape(hidden_halves),
+        grad_gate.reshape(hidden_halves),
+        grad_up.reshape(hidden_halves),
+        gate,
+        up,
+        down,
+        cotangent.reshape(halves),
+        middle,
+        gain.reshape(1, model_width),
+    )
+    return (
+        grad_attend.reshape(rows, model_width),
+        layer.reshape(rows, model_width),
+        grad_middle,
+        sums,
+    )
+
+
+def input_kernel(
+    size,
+    partial,
+    tokens,
+    grad_middle,
+    gain,
+    grad_out,
+    sum_out,
+    own,
+    held,
+    out,
+    stream,
+    grad_mid,
+    sems,
+    load_sems,
+    save_sems,
+):
+    half_rows = own.shape[1]
+    chunks = half_rows // CHUNK
+    line = Line(size, chunks, own, held, out, sems)
+    half = line.end_half
+    loads = load_all(
+        [(partial, own), (tokens.at[half], stream), (grad_middle, grad_mid)], load_sems
+    )
+    for load in loads:
+        load.start()
+    sum_out[...] = jnp.zeros_like(sum_out)
+    line.enter()
+    for load in loads:
+        load.wait()
+
+    def finish(chunk, total):
+        rows = chunk_rows(chunk)
+        values = stream[rows].astype(jnp.float32)
+        scale = inverse_rms(values)
+        weighted = total * gain[...]
+        inner = jnp.mean(weighted * values, axis=-1, keepdims=True)
+        grad = grad_mid[rows] + scale * weighted - values * (scale * scale * scale * inner)
+        sum_out[...] += fold_rows(total * (values * scale))
+        out[half, rows] = grad.astype(jnp.bfloat16)
+
+    def save(which, chunk):
+        rows = chunk_rows(chunk)
+        return pltpu.make_async_copy(
+            out.at[which, rows], grad_out.at[which, rows], save_sems.at[which, chunk]
+        )
+
+    def arrived(which, chunk):
+        save(which, chunk).start()
+
+    @pl.loop(0, chunks + 2 * (size - 1))
+    def _(step):
+        line.slot(step, finish, arrived)
+
+    @pl.loop(0, chunks)
+    def _(chunk):
+        for which in (0, 1):
+            save(which, chunk).wait()
+
+    line.leave()
+
+
+def input_block(partial, tokens, grad_middle, gain, size):
+    rows, model_width = partial.shape
+    half_rows = rows // 2
+    low = jnp.bfloat16
+    chunks = half_rows // CHUNK
+    anywhere = pl.BlockSpec(memory_space=pl.ANY)
+    local_spec = pl.BlockSpec(memory_space=pltpu.VMEM)
+    halves = (2, half_rows, model_width)
+    grad_input, sums = pl.pallas_call(
+        lambda *refs: input_kernel(size, *refs),
+        out_shape=(
+            jax.ShapeDtypeStruct(halves, low),
+            jax.ShapeDtypeStruct((8, model_width), jnp.float32),
+        ),
+        in_specs=[anywhere] * 3 + [local_spec],
+        out_specs=[anywhere, local_spec],
+        scratch_shapes=[
+            pltpu.VMEM(halves, low),
+            pltpu.VMEM(halves, low),
+            pltpu.VMEM(halves, low),
+            pltpu.VMEM((half_rows, model_width), low),
+            pltpu.VMEM((half_rows, model_width), jnp.float32),
+            pltpu.SemaphoreType.DMA((4, 2, chunks)),
+            pltpu.SemaphoreType.DMA((3,)),
+            pltpu.SemaphoreType.DMA((2, chunks)),
+        ],
+        compiler_params=pltpu.CompilerParams(
+            collective_id=3, has_side_effects=True, vmem_limit_bytes=VMEM_BYTES
+        ),
+        cost_estimate=pl.CostEstimate(flops=0, bytes_accessed=300000000, transcendentals=0),
+        name="input_block",
+    )(
+        partial.reshape(halves),
+        tokens.reshape(halves),
+        grad_middle,
+        gain.reshape(1, model_width),
+    )
+    return grad_input.reshape(rows, model_width), sums
 
 
 def local(
@@ -115,13 +839,9 @@
     score_shift = math.log(seq_len)
     shape_heads = (seq_count, block_len, heads_here, HD)
     low = jnp.bfloat16
-    part_rows = row_count // tp_size
-    row_at = lax.axis_index("tp") * part_rows
 
     token_rows = tokens.reshape(row_count, model_width)
     grad_rows = cotangent.reshape(row_count, model_width)
-    token_part = lax.dynamic_slice_in_dim(token_rows, row_at, part_rows, 0).astype(jnp.float32)
-    cotangent_part = lax.dynamic_slice_in_dim(grad_rows, row_at, part_rows, 0).astype(jnp.float32)
 
     qkv_full = spread_rows(jnp.concatenate([w_query, w_key, w_value], axis=1), ctx_size)
     gains = lax.all_gather(jnp.stack([gain_attend, gain_feed]), "fsdp", axis=1, tiled=True)
@@ -171,29 +891,10 @@
     )
     mixed_rows = attended.reshape(row_count, width_here).astype(low)
 
-    attend_part = sum_rows(plain_dot(mixed_rows, output_full))
-    middle = token_part + attend_part
-    scale_two = inverse_rms(middle)
-    normed_two = every_row((middle * scale_two * gain_two).astype(low))
-
-    gate_vals = plain_dot(normed_two, gate_full)
-    up_vals = plain_dot(normed_two, up_full)
-    gate_sig = jax.nn.sigmoid(gate_vals)
-    gate_act = gate_vals * gate_sig
-    hidden = (gate_act * up_vals).astype(low)
-    grad_hidden = dot_last(grad_rows, down_full)
-    slope = gate_sig * (1.0 + gate_vals * (1.0 - gate_sig))
-    grad_gate = (grad_hidden * up_vals * slope).astype(low)
-    grad_up = (grad_hidden * gate_act).astype(low)
-    grad_normed_two = sum_rows(dot_last(grad_gate, gate_full) + dot_last(grad_up, up_full))
-
-    feed_part = sum_rows(plain_dot(hidden, down_full))
-    result = middle + feed_part
-    layer_out = every_row(result.astype(low)).reshape(tokens.shape)
-
-    grad_middle_norm, grad_gain_two = norm_back(grad_normed_two, middle, scale_two, gain_two)
-    grad_middle = cotangent_part + grad_middle_norm
-    grad_attend = every_row(grad_middle.astype(low))
+    attend_part = plain_dot(mixed_rows, output_full).astype(low)
+    normed_two, hidden, grad_gate, grad_up, middle, attend_squares = feed_block(
+        attend_part, token_rows, grad_rows, gate_full, up_full, down_full, gain_two, tp_size
+    )
 
     def scatter(value, dimension):
         return lax.psum_scatter(
@@ -203,6 +904,20 @@
     grad_down = scatter(dot_first(hidden, grad_rows), 1)
     grad_gate_w = scatter(dot_first(normed_two, grad_gate), 0)
     grad_up_w = scatter(dot_first(normed_two, grad_up), 0)
+
+    grad_attend, layer_rows, grad_middle, feed_sums = back_block(
+        hidden,
+        grad_gate,
+        grad_up,
+        gate_full,
+        up_full,
+        down_full,
+        grad_rows,
+        middle,
+        gain_two,
+        tp_size,
+    )
+    layer_out = layer_rows.reshape(tokens.shape)
 
     grad_mixed = dot_last(grad_attend, output_full).astype(low)
     grad_output_w = scatter(dot_first(mixed_rows, grad_attend), 1)
@@ -240,17 +955,15 @@
         ],
         axis=1,
     )
-    grad_normed_one = sum_rows(dot_last(grad_qkv, qkv_full))
     grad_qkv_w = scatter(dot_first(normed_one, grad_qkv), 0)
-    scale_one_part = lax.dynamic_slice_in_dim(scale_one, row_at, part_rows, 0)
-    grad_input_norm, grad_gain_one = norm_back(
-        grad_normed_one, token_part, scale_one_part, gain_one
-    )
-    grad_input = every_row((grad_middle + grad_input_norm).astype(low)).reshape(tokens.shape)
-
-    sums = jnp.stack(
-        [jnp.sum(result * result), jnp.sum(attend_part * attend_part), jnp.sum(feed_part * feed_part)]
-    )
+    input_rows, input_sums = input_block(
+        dot_last(grad_qkv, qkv_full).astype(low), token_rows, grad_middle, gain_one, tp_size
+    )
+    grad_input = input_rows.reshape(tokens.shape)
+
+    grad_gain_one = jnp.sum(input_sums, axis=0)
+    grad_gain_two = jnp.sum(feed_sums[0], axis=0)
+    sums = jnp.stack([jnp.sum(feed_sums[1]), jnp.sum(attend_squares), jnp.sum(feed_sums[2])])
     small = lax.psum(
         jnp.concatenate([grad_gain_one, grad_gain_two, sums]), ("fsdp", "ctx", "tp")
     )

time: 1560 us -> 1250 us (0.80)
  waiting for transfers between devices: 1110 us -> 425 us
  Pallas kernels: 0 us -> 462 us
  matrix products: 233 us -> 147 us
    pallas_call x0 -> x3, Pallas kernels: none -> 462 us  [the longest x1 217 us: back_block(): pl.pallas_call(lambda *refs: back_kernel(size, *refs), out_shape=(jax.Sha...]
    all_gather x4 -> x0, waiting for transfers between devices: 324 us -> none  [every_row(): return lax.all_gather(rows, 'tp', axis=0, tiled=True)]
    reduce_scatter x4 -> x0, waiting for transfers between devices: 229 us -> none  [sum_rows(): lax.psum_scatter(partial.astype(jnp.bfloat16), 'tp', scatter_dimension=0,...]
    reduce_scatter x1, waiting for transfers between devices: 61.7 us -> 9.74 us  [local(): lax.psum_scatter(pair, 'ctx', scatter_dimension=1, tiled=True)]
    reduce_scatter x5, waiting for transfers between devices: 277 us -> 230 us  [scatter(): lax.psum_scatter(value.astype(low), ('fsdp', 'ctx'), scatter_dimension=di...]
    dot_general x5 -> x2, matrix products: 59.2 us -> 16.2 us  [dot_last(): lax.dot_general(left_side, right_side, (((1,), (1,)), ((), ())), preferre...]
    dot_general x5 -> x2, matrix products: 59.6 us -> 16.8 us  [plain_dot(): return jnp.dot(left_side, right_side, preferred_element_type=jnp.float32)]
    reshape x0 -> x1, local copies, waits for them, and re-layouts: none -> 16.4 us  [spread_columns(): held = held.reshape(fsdp_size, piece.shape[0], piece.shape[1])]
  transfers between devices with their start and end apart: 20 -> 12, of which waited for: 19 -> 10; matrix products, arithmetic and copies ran while one was open for 12% -> 18% of each run, Pallas kernels for 0% -> 10%
where the time goes in v2:
time: 1250 us; the launch traced here: 1240 us
  Pallas kernels  462 us (37%)
  waiting for transfers between devices  425 us (34%)
  matrix products  147 us (12%)
  local copies, waits for them, and re-layouts  94.9 us (8%)
  blocking collectives  49.8 us (4%)
  other arithmetic  41.7 us (3%)
  between operations  14.9 us (1%)
    reduce_scatter x5, waiting for transfers between devices, scatter(): lax.psum_scatter(value.astype(low), ('fsdp', 'ctx'), scatter_dimension=di...  230 us
    pallas_call x1, Pallas kernels, back_block(): pl.pallas_call(lambda *refs: back_kernel(size, *refs), out_shape=(jax.Sha...  217 us
    pallas_call x1, Pallas kernels, feed_block(): pl.pallas_call(lambda *refs: feed_kernel(size, *refs), out_shape=(jax.Sha...  125 us
    pallas_call x1, Pallas kernels, input_block(): pl.pallas_call(lambda *refs: input_kernel(size, *refs), out_shape=(jax.Sh...  120 us
    all_gather x3, waiting for transfers between devices, spread_rows(): return lax.all_gather(mine, ('fsdp', 'ctx'), axis=0, tiled=True)  111 us
    dot_general x5, matrix products, dot_first(): lax.dot_general(left_side, right_side, (((0,), (0,)), ((), ())), preferre...  60.1 us
    all_gather x2, waiting for transfers between devices, spread_columns(): held = lax.all_gather(mine, ('fsdp', 'ctx'), axis=0, tiled=True)  39.7 us
    psum x1, blocking collectives, local(): lax.psum(jnp.concatenate([grad_gain_one, grad_gain_two, sums]), ('fsdp',...  39.3 us
  transfers between devices with their start and end apart: 12, of which 10 were waited for; matrix products, arithmetic and copies ran while one was open for 18% of the time, Pallas kernels for 10%

profile of v2, /device:TPU:0, one launch (start us, length us, event | category | flops | bytes accessed | tf_op | source)
XLA Modules:
  0.0 1236.2 jit_solution(16273273763285392757)
XLA Ops:
  7.3 2.1 fusion.10
  9.4 1.7 constant_dynamic-slice_fusion.3
  11.1 2.3 constant_dynamic-slice_fusion
  13.6 3.2 multiply_reduce_fusion
  16.9 5.3 all_gather.24
  22.2 1.9 multiply_cosine_fusion
  25.4 3.0 fusion.1
  28.4 30.2 %all-gather.7.cloned.1.call-done = bf16[2048,1536]{1,0:T(8,128)(2,1)} async-done(((bf16[256,1536]{1,0:T(8,128)(2,1)}), bf16[2048,1536]{1,0:T(8,128)(2,1)}) %all-gather.7.cloned.1.call-update) | async-done | bytes 6291472 | tf_op jit(solution)/shard_map/all_gather | solution.py:72
  58.6 10.0 fusion.27
  69.7 2.4 fusion.19
  72.2 1.9 reshape.148
  74.1 2.3 copy.65
  76.4 2.9 reshape.145
  79.2 4.7 fusion.21
  83.9 2.7 subtract_convert_fusion.2
  89.8 2.3 constant_dynamic-slice_fusion.2
  92.2 2.4 constant_dynamic-slice_fusion.1
  94.6 5.2 all_gather.27
  101.5 3.9 copy.70
  105.4 39.6 %all-gather.17.cloned.1.call-done = bf16[4096,1024]{1,0:T(8,128)(2,1)} async-done(((bf16[512,1024]{1,0:T(8,128)(2,1)}), bf16[4096,1024]{1,0:T(8,128)(2,1)}) %all-gather.17.cloned.1.call-update) | async-done | bytes 8388624 | tf_op jit(solution)/shard_map/all_gather | solution.py:78
  145.1 16.4 %copy.71 = bf16[2,2048,1024]{2,0,1:T(2,128)(2,1)} copy(bf16[2,2048,1024]{2,1,0:T(8,128)(2,1)} %bitcast.103) | data formatting | bytes 16777216 | tf_op jit(solution)/shard_map/reshape | solution.py:80
  161.4 10.3 copy.98
  171.8 34.7 %all-gather.9.cloned.1.call-done = bf16[4,1024,1024]{1,2,0:T(8,128)(2,1)} async-done(((bf16[4,256,1024]{1,2,0:T(8,128)(2,1)}), bf16[4,1024,1024]{1,2,0:T(8,128)(2,1)}) %all-gather.9.cloned.1.call-update) | async-done | bytes 8388624 | tf_op jit(solution)/shard_map/all_gather | solution.py:866
  206.5 4.1 fusion.18
  210.6 8.8 add_divide_fusion
  219.3 10.0 fusion.4
  229.4 1.8 copy.69
  231.2 6.8 convolution_convert_fusion.3
  238.0 24.5 %all-gather.13.cloned.1.call-done.refs_3_ = bf16[2048,2048]{1,0:T(8,128)(2,1)} async-done(((bf16[256,2048]{1,0:T(8,128)(2,1)}), bf16[2048,2048]{1,0:T(8,128)(2,1)}) %all-gather.13.cloned.1.call-update) | async-done | bytes 8388624 | tf_op jit(solution)/shard_map/all_gather | solution.py:72
  262.5 56.0 %all-gather.15.cloned.1.call-done.refs_4_ = bf16[2048,2048]{1,0:T(8,128)(2,1)} async-done(((bf16[256,2048]{1,0:T(8,128)(2,1)}), bf16[2048,2048]{1,0:T(8,128)(2,1)}) %all-gather.15.cloned.1.call-update) | async-done | bytes 8388624 | tf_op jit(solution)/shard_map/all_gather | solution.py:72
  318.5 125.1 %feed_block.1 = (bf16[2,512,2048]{2,1,0:T(8,128)(2,1)}, bf16[2,512,2048]{2,1,0:T(8,128)(2,1)}, bf16[2,512,2048]{2,1,0:T(8,128)(2,1)}, bf16[2,512,2048]{2,1,0:T(8...) custom-call(bf16[2,512,2048]{2,1,0:T(8,128)(2,1)} %bitcast.132, bf16[2,512,2048]{2,1,0:T(8,128)(2,1)} %bitcast.93, ...), custom_call_target="tpu_custom_call" | custom-call | flops 25769803776 | bytes 300000000 | tf_op jit(solution)/shard_map/feed_block/pallas_call | solution.py:390
  443.6 217.1 %back_block.1 = (bf16[2,512,2048]{2,1,0:T(8,128)(2,1)}, bf16[2,512,2048]{2,1,0:T(8,128)(2,1)}, f32[512,2048]{1,0:T(8,128)}, f32[3,8,2048]{2,1,0:T(8,128)}) custom-call(bf16[2,512,2048]{2,1,0:T(8,128)(2,1)} %get-tuple-element.26.refs_0_, bf16[2,512,2048]{2,1,0:T(8,128)(2,1)} %get-tuple-element.27.refs_1_, bf16[2,512,2048]{2,1,0:T(8,128)(2,1)} %get-tuple-element.28.refs_2_, ...), custom_call_target="tpu_custom_call" | custom-call | flops 25769803776 | bytes 600000000 | tf_op jit(solution)/shard_map/back_block/pallas_call | solution.py:661
  660.7 5.2 convolution_convert_fusion.6
  668.6 9.7 select_convert_fusion
  678.3 12.7 %convolution_convert_fusion.5 = bf16[4,4,128,1024]{3,2,1,0:T(8,128)(2,1)} fusion(bf16[4,256,4,128]{1,3,2,0:T(8,128)(2,1)S(1)} %copy.77, f32[4,4,256,1024]{3,2,1,0:T(8,128)} %add_divide_fusion, pred[4,256,1024]{2,1,0:T(8,128)(4,1)S(1)} %copy-done.3), kind=kOutput, calls=%fused_computation.20 | convolution fusion | flops 1080033280 | bytes 23068672 | tf_op jit(solution)/shard_map/shqk,sqhd->skhd/dot_general | solution.py:935
  690.9 5.9 multiply_convert_fusion
  696.9 7.7 pad_maximum_fusion
  705.8 6.4 convolution_convert_fusion.4
  712.3 15.7 %bitcast_convert_fusion = bf16[2048,2048]{1,0:T(8,128)(2,1)} fusion(bf16[2,512,2048]{2,1,0:T(8,128)(2,1)} %get-tuple-element.37, bf16[2,512,2048]{2,1,0:T(8,128)(2,1)} %get-tuple-element.28.refs_2_), kind=kOutput, calls=%fused_computation | convolution fusion | flops 8594128896 | bytes 16777216 | tf_op jit(solution)/shard_map/dot_general | solution.py:28
  728.1 14.5 %bitcast_convert_fusion.1 = bf16[2048,2048]{1,0:T(8,128)(2,1)} fusion(bf16[2,512,2048]{2,1,0:T(8,128)(2,1)} %get-tuple-element.37, bf16[2,512,2048]{2,1,0:T(8,128)(2,1)} %get-tuple-element.27.refs_1_), kind=kOutput, calls=%fused_computation.1 | convolution fusion | flops 8594128896 | bytes 16777216 | tf_op jit(solution)/shard_map/dot_general | solution.py:28
  742.6 14.0 %convolution_convert_fusion = bf16[2048,2048]{1,0:T(8,128)(2,1)} fusion(bf16[1024,2048]{1,0:T(8,128)(2,1)} %bitcast.129, bf16[1024,2048]{1,0:T(8,128)(2,1)} %bitcast.128), kind=kOutput, calls=%fused_computation.11 | convolution fusion | flops 8594128896 | bytes 16777216 | tf_op jit(solution)/shard_map/dot_general | solution.py:28
  756.7 7.0 multiply_bitcast_fusion
  763.7 9.7 reduce-scatter.7.cloned.1.call-done
  773.5 2.6 fusion.20
  776.1 2.4 copy.81
  780.1 3.2 copy.94
  783.3 3.2 copy.95
  786.6 3.3 subtract_convert_fusion.1
  794.0 9.4 convolution_convert_fusion.1
  805.5 12.9 %reduce-scatter.11.cloned.1.call-done = bf16[512,256]{1,0:T(8,128)(2,1)} async-done(((bf16[512,2048]{1,0:T(8,128)(2,1)}), bf16[512,256]{1,0:T(8,128)(2,1)}) %reduce-scatter.11.cloned.1.call-update) | async-done | bytes 262160 | tf_op jit(solution)/shard_map/reduce_scatter | solution.py:900
  818.5 1.8 convert_element_type.144
  820.2 73.2 %reduce-scatter.15.cloned.1.call-done = bf16[256,2048]{1,0:T(8,128)(2,1)} async-done(((bf16[2048,2048]{1,0:T(8,128)(2,1)}), bf16[256,2048]{1,0:T(8,128)(2,1)}) %reduce-scatter.15.cloned.1.call-update) | async-done | bytes 1048592 | tf_op jit(solution)/shard_map/reduce_scatter | solution.py:900
  893.5 2.8 convert_element_type.148
  896.3 72.0 %reduce-scatter.13.cloned.1.call-done = bf16[256,2048]{1,0:T(8,128)(2,1)} async-done(((bf16[2048,2048]{1,0:T(8,128)(2,1)}), bf16[256,2048]{1,0:T(8,128)(2,1)}) %reduce-scatter.13.cloned.1.call-update) | async-done | bytes 1048592 | tf_op jit(solution)/shard_map/reduce_scatter | solution.py:900
  968.3 2.8 convert_element_type.146
  971.1 72.0 %reduce-scatter.17.cloned.1.call-done = bf16[2048,256]{1,0:T(8,128)(2,1)} async-done(((bf16[2048,2048]{1,0:T(8,128)(2,1)}), bf16[2048,256]{1,0:T(8,128)(2,1)}) %reduce-scatter.17.cloned.1.call-update) | async-done | bytes 1048592 | tf_op jit(solution)/shard_map/reduce_scatter | solution.py:900
  1043.1 2.7 convert_element_type.150
  1045.8 11.0 convolution_convert_fusion.2
  1056.8 119.7 %input_block.1 = (bf16[2,512,2048]{2,1,0:T(8,128)(2,1)}, f32[8,2048]{1,0:T(8,128)}) custom-call(bf16[2,512,2048]{2,1,0:T(8,128)(2,1)} %bitcast.112, bf16[2,512,2048]{2,1,0:T(8,128)(2,1)} %bitcast.94, f32[512,2048]{1,0:T(8,128)} %get-tuple-element.32.refs_2_, f32[1,2048]{1,0:T(1,128)} %copy-done.18), custom_call_target="tpu_custom_call" | custom-call | bytes 300000000 | tf_op jit(solution)/shard_map/input_block/pallas_call | solution.py:784
  1177.3 2.0 concatenate.39
  1179.4 39.3 %psum.7 = f32[4099]{0:T(1024)S(1)} all-reduce(f32[4099]{0:T(1024)S(1)} %concatenate.39), channel_id=1, replica_groups=mesh['fsdp'=2,'ctx'=4,'tp'=4] {'fsdp','ctx','tp'}, use_global_device_ids=true, to_apply=%region_7.8 | all-reduce | flops 4099 | bytes 32792 | tf_op jit(solution)/shard_map/psum | solution.py:967
  1219.9 2.3 fusion.24
  1222.2 4.9 copy.123
  1227.1 2.0 copy.124
  (102 shorter events, 21.4 us)
Async XLA Ops:
  7.2 51.4 %all-gather.7.cloned.1.call-start = ((), (), s32[]{:S(2)}) async-start(), calls=%async_computation.6 | async-start | bytes 7077888 | tf_op jit(solution)/shard_map/all_gather | solution.py:72
  7.2 6.3 copy-start.21
  7.2 6.3 copy-start.22
  7.3 6.4 copy-start.23
  9.3 92.1 %all-gather.11.cloned.1.call-start = ((), (), s32[]{:S(2)}) async-start(), calls=%async_computation.8 | async-start | bytes 2359296 | tf_op jit(solution)/shard_map/all_gather | solution.py:78
  11.1 134.0 %all-gather.17.cloned.1.call-start = ((), (), s32[]{:S(2)}) async-start(), calls=%async_computation.11 | async-start | bytes 9437184 | tf_op jit(solution)/shard_map/all_gather | solution.py:78
  13.5 193.0 %all-gather.9.cloned.1.call-start = ((), (), s32[]{:S(2)}) async-start(), calls=%async_computation.7 | async-start | bytes 10485760 | tf_op jit(solution)/shard_map/all_gather | solution.py:866
  13.6 11.8 copy-start.1
  24.1 59.8 %copy-start.5 = (f32[4,256,64]{2,1,0:T(8,128)}, f32[4,256,64]{2,1,0:T(8,128)S(1)}, u32[]{:S(2)}) copy-start(f32[4,256,64]{2,1,0:T(8,128)S(1)} %get-tuple-element.72) | copy-start | bytes 786436
  24.1 59.8 %copy-start.7 = (f32[4,256,64]{2,1,0:T(8,128)}, f32[4,256,64]{2,1,0:T(8,128)S(1)}, u32[]{:S(2)}) copy-start(f32[4,256,64]{2,1,0:T(8,128)S(1)} %get-tuple-element.73) | copy-start | bytes 786436
  24.8 0.6 copy-start.18
  86.6 1.2 copy-start.13
  89.3 5.2 copy-start.20
  89.4 173.1 %all-gather.13.cloned.1.call-start = ((), (), s32[]{:S(2)}) async-start(), calls=%async_computation.9 | async-start | bytes 9437184 | tf_op jit(solution)/shard_map/all_gather | solution.py:72
  92.1 226.4 %all-gather.15.cloned.1.call-start = ((), (), s32[]{:S(2)}) async-start(), calls=%async_computation.10 | async-start | bytes 9437184 | tf_op jit(solution)/shard_map/all_gather | solution.py:72
  94.5 678.9 %reduce-scatter.7.cloned.1.call-start = ((), (), s32[]{:S(2)}) async-start(), calls=%async_computation.12 | async-start | bytes 10485760 | tf_op jit(solution)/shard_map/reduce_scatter | solution.py:945
  206.4 4.1 copy-start.9
  206.5 4.1 copy-start.10
  210.5 8.8 copy-start.4
  210.5 8.8 copy-start.2
  231.2 6.8 copy-start.15
  665.9 2.6 copy-start.3
  678.2 12.7 %copy-start = (bf16[4,4,256,1024]{3,2,1,0:T(8,128)(2,1)}, bf16[4,4,256,1024]{3,2,1,0:T(8,128)(2,1)S(1)}, u32[]{:S(2)}) copy-start(bf16[4,4,256,1024]{3,2,1,0:T(8,128)(2,1)S(1)} %select_convert_fusion) | copy-start | bytes 25165828
  704.6 1.2 copy-start.16
  704.6 113.9 %reduce-scatter.11.cloned.1.call-start = ((), (), s32[]{:S(2)}) async-start(), calls=%async_computation.14 | async-start | bytes 2359296 | tf_op jit(solution)/shard_map/reduce_scatter | solution.py:900
  712.2 181.3 %reduce-scatter.15.cloned.1.call-start = ((), (), s32[]{:S(2)}) async-start(), calls=%async_computation.16 | async-start | bytes 9437184 | tf_op jit(solution)/shard_map/reduce_scatter | solution.py:900
  728.0 240.3 %reduce-scatter.13.cloned.1.call-start = ((), (), s32[]{:S(2)}) async-start(), calls=%async_computation.15 | async-start | bytes 9437184 | tf_op jit(solution)/shard_map/reduce_scatter | solution.py:900
  742.6 300.5 %reduce-scatter.17.cloned.1.call-start = ((), (), s32[]{:S(2)}) async-start(), calls=%async_computation.17 | async-start | bytes 9437184 | tf_op jit(solution)/shard_map/reduce_scatter | solution.py:900
  756.7 463.2 %reduce-scatter.9.cloned.1.call-start = ((), (), s32[]{:S(2)}) async-start(), calls=%async_computation.13 | async-start | bytes 7077888 | tf_op jit(solution)/shard_map/reduce_scatter | solution.py:900
  780.1 6.5 copy-start.6
  780.1 6.5 copy-start.8
  791.5 2.2 copy-start.11
  791.5 2.5 copy-start.14
  803.4 0.8 copy-start.19
  803.4 1.5 copy-start.17
  1222.2 4.9 copy-start.12
Sparse Core Ops, SparseCore 0:
  10.4 48.1 all-gather.6
  61.1 27.7 all-gather.10
  90.8 54.2 all-gather.16
  147.0 59.3 all-gather.8
  208.2 54.2 all-gather.12
  264.2 54.2 all-gather.14
  704.7 68.6 reduce-scatter.6
  777.3 41.0 reduce-scatter.10
  821.9 71.5 reduce-scatter.14
  896.8 71.4 reduce-scatter.12
  971.8 71.2 reduce-scatter.16
  1046.3 61.7 reduce-scatter.8
